TPU v7x, 128 devices: a whole 4x4x4 slice. The times are simulated.
128 devices in a mesh: genes: 64 (over z, y, x_hi, core), cols: 2 (over x_lo).
Axes of the slice: x: 4 (x_hi: 2, x_lo: 2; x = x_hi * 2 + x_lo), y: 4, z: 4, core: 2. Of those that a mesh axis runs over, the one named last changes fastest.
Arguments:
- expression: float32 [384, 40960], P(None, ('genes', 'cols')), may hold values from -200 to 200
- resample: int32 [384], replicated, may hold values from 0 to 383
- labels: int32 [40960, 300], P(('genes', 'cols')), may hold values from 0 to 1, as said below
- ref_kim: float32 [40960], P(('genes', 'cols')), may hold values from 0 to 1
Outputs:
- connectivity: float32 [40960, 300], P(('genes', 'cols'))
- preservation: float32 [2, 300], replicated
Inputs may be any that keep to these rules, and one draw needn't show every extreme that they name: `labels`: each row holds exactly one 1; every module has 32 or more genes.
All inputs are finite; a program needn't handle non-finite values.
Results may differ from a plain program's by a relative error of at most 0.0031.
Values may be sent and summed in bfloat16 or wider, within the bound.
A program may use at most 64 MiB of HBM per device.

v0:
```python
import math

import jax
import jax.numpy as jnp
from jax import lax
from jax.sharding import Mesh
from jax.sharding import PartitionSpec as P

G = 40960
GENES = ("genes_0", "genes_1", "genes_2", "genes_3")
GENES_COLS = ("genes_0", "genes_1", "genes_2", "genes_3", "cols")


def in_order(blocks, dim):
    lengths = list(blocks.shape[1:])
    lengths[dim] *= blocks.shape[0]
    return jnp.moveaxis(blocks, 0, dim).reshape(lengths)


def sent_to_all(x, axis):
    copies = jnp.broadcast_to(x, (lax.axis_size(axis), *x.shape))
    return lax.all_to_all(copies, axis, split_axis=0, concat_axis=0, tiled=True)


def gathered_copies(x, axis, dim):
    return in_order(sent_to_all(x, axis), dim)


def split_up(x, dim, count):
    before, after = (x.shape[:dim], x.shape[dim + 1 :])
    return jnp.moveaxis(x.reshape(*before, count, -1, *after), dim, 0)


def sum_at_owner(x, axis, dim):
    count = lax.axis_size(axis)
    blocks = lax.all_to_all(split_up(x, dim, count), axis, 0, 0, tiled=True)
    return jnp.sum(blocks.astype(jnp.float32), axis=0)


def one_axis_at_a_time(x, axes):
    for axis in axes:
        x = lax.psum(x, axis)
    return x


def standardize(expression, resample):
    boot = jnp.take(expression, resample, axis=0)
    centered = boot - jnp.mean(boot, axis=0, keepdims=True)
    total = jnp.sum(centered * centered, axis=0, keepdims=True)
    return (centered * lax.rsqrt(total + 1e-06)).astype(jnp.bfloat16)


def local_sums(connectivity, labels, ref_kim):
    member = labels.astype(jnp.float32)
    kim = jnp.sum(connectivity * member, axis=1)
    rowsum = jnp.sum(connectivity, axis=1)
    stacked = jnp.stack(
        [kim, kim * kim, ref_kim, ref_kim * ref_kim, kim * ref_kim, rowsum, jnp.ones_like(kim)],
        axis=1,
    )
    return jnp.dot(
        member.T, stacked, precision=lax.Precision.HIGHEST, preferred_element_type=jnp.float32
    )


def preserve(sums, total_genes):
    counts = sums[:, 6]
    mean_x = sums[:, 0] / (counts * counts)
    var_x = jnp.maximum(sums[:, 1] / (counts * counts * counts) - mean_x * mean_x, 0.0001)
    mean_y = sums[:, 2] / counts
    var_y = jnp.maximum(sums[:, 3] / counts - mean_y * mean_y, 0.01)
    cross = sums[:, 4] / (counts * counts) - mean_x * mean_y
    between = (sums[:, 5] - sums[:, 0]) / (counts * (total_genes - counts))
    density = (mean_x - between) * jnp.sqrt(counts / var_x)
    linked = cross * jnp.sqrt(counts / (var_x * var_y))
    return jnp.stack([density, linked], axis=0)


def tile_term(row_block, column_block, column_ids, module_count):
    scores = lax.dot_general(
        row_block, column_block, (((0,), (0,)), ((), ())), preferred_element_type=jnp.float32
    )
    squares = scores * scores
    adjacency = (squares * squares * squares).astype(jnp.bfloat16)
    member_block = (
        column_ids[:, None] == jnp.arange(module_count, dtype=jnp.int32)[None, :]
    ).astype(jnp.bfloat16)
    return jnp.dot(adjacency, member_block, preferred_element_type=jnp.float32)


def add_tiles(carried, row_block, piece, every_ids, shard_width, module_count):
    span_width = piece.shape[1]
    column_step = shard_width * math.gcd(span_width // shard_width, 8)
    steps_total = span_width // column_step

    def one_step(step_index, accumulated):
        columns = lax.dynamic_slice_in_dim(piece, step_index * column_step, column_step, 1)
        column_ids = lax.dynamic_slice_in_dim(every_ids, step_index * column_step, column_step, 0)
        return accumulated + tile_term(row_block, columns, column_ids, module_count)

    return lax.fori_loop(0, steps_total, one_step, carried)


def local(expression, resample, labels, ref_kim):
    scaled = standardize(expression, resample)
    module_count = labels.shape[1]
    shard_width = scaled.shape[1]
    module_ids = jnp.sum(labels * jnp.arange(module_count, dtype=jnp.int32)[None, :], axis=1)
    row_block = gathered_copies(scaled, "cols", 1)
    panel_ids = gathered_copies(module_ids, GENES, 0)
    initial = jnp.zeros((row_block.shape[1], module_count), jnp.float32)
    partial_value = add_tiles(
        initial,
        row_block,
        lax.all_gather(scaled, GENES, axis=1, tiled=True),
        panel_ids,
        shard_width,
        module_count,
    )
    connectivity = sum_at_owner(partial_value.astype(jnp.bfloat16), "cols", 0)
    sums = one_axis_at_a_time(local_sums(connectivity, labels, ref_kim), GENES_COLS)
    return (connectivity, preserve(sums, G))


def solution(mesh):
    torus = Mesh(
        mesh.devices.reshape(4, 4, 2, 2, mesh.shape["cols"]),
        ("genes_0", "genes_1", "genes_2", "genes_3", "cols"),
    )
    placed = (P(None, GENES_COLS), P(), P(GENES_COLS, None), P(GENES_COLS))
    return jax.shard_map(
        local, mesh=torus, in_specs=placed, out_specs=(P(GENES_COLS, None), P()), check_vma=False
    )
```

profile of v0, /device:TPU:1, one launch (start us, length us, event | category | flops | bytes accessed | tf_op | source)
XLA Modules:
  0.0 232.8 jit_solution(9748620751659558973)
XLA Ops:
  8.6 1.3 copy.21
  9.9 1.7 gather_fusion
  12.3 0.9 multiply_convert_fusion
  13.3 22.0 %all_to_all.16 = s32[64,1,320]{2,1,0:T(1,128)S(1)} all-to-all(s32[64,1,320]{2,1,0:T(1,128)S(1)} %broadcast_in_dim.35), channel_id=1, replica_groups=mesh['genes_0'=4,'genes_1'=4,'genes_2'=2,'genes_3'=2,'cols'=2] {'genes_0..., dimensions={0} | all-to-all | bytes 163840 | tf_op jit(solution)/shard_map/all_to_all | solution.py:22
  35.3 1.8 broadcast_in_dim.34
  37.0 3.5 %all-to-all-start = ((bf16[2,384,320]{1,2,0:T(8,128)(2,1)}), bf16[2,384,320]{1,2,0:T(8,128)(2,1)S(1)}, u32[]{:S(2)}, u32[]{:S(2)}) async-start(bf16[2,384,320]{1,2,0:T(8,128)(2,1)} %broadcast_in_dim.34), calls=%async_computation | async-start | bytes 983040 | tf_op jit(solution)/shard_map/all_to_all | solution.py:22
  40.9 6.8 %all-to-all-done = bf16[2,384,320]{1,2,0:T(8,128)(2,1)S(1)} async-done(((bf16[2,384,320]{1,2,0:T(8,128)(2,1)}), bf16[2,384,320]{1,2,0:T(8,128)(2,1)S(1)}, u32[]{:S(2)}, u32[]{:S(2)}) %all-to-all-start) | async-done | bytes 491552 | tf_op jit(solution)/shard_map/all_to_all | solution.py:22
  48.0 70.7 %all-gather.2.cloned.1.call-done = bf16[384,20480]{0,1:T(8,128)(2,1)} async-done(((bf16[384,320]{0,1:T(8,128)(2,1)}), bf16[384,20480]{0,1:T(8,128)(2,1)}) %all-gather.2.cloned.1.call-update) | async-done | bytes 15728656 | tf_op jit(solution)/shard_map/all_gather | solution.py:115
  118.7 43.6 %while.14 = (s32[]{:T(128)}, f32[640,300]{0,1:T(8,128)S(1)}, bf16[384,20480]{0,1:T(8,128)(2,1)}, bf16[384,640]{1,0:T(8,128)(2,1)S(1)}, s32[20480]{0:T(1024)S(1)}...) while((s32[]{:T(128)}, f32[640,300]{0,1:T(8,128)S(1)}, bf16[384,20480]{0,1:T(8,128)(2,1)}, ...), condition=%wide.region_4.5_spmd.clone, body=%wide.region_3.4_spmd.clone.sunk | while | flops 2249036800 | bytes 4024477 | solution.py:101
  118.7 5.3 %fusion.32 = f32[640,300]{0,1:T(8,128)S(1)} fusion(s32[2560]{0:T(1024)S(1)} %dynamic_slice.25, bf16[384,640]{1,0:T(8,128)(2,1)S(1)} %get-tuple-element.204, bf16[384,20480]{0,1:T(8,128)(2,1)} %get-tuple-element.203, s32[]{:T(128)S(6)} %select_n.27, f32[640,300]{0,1:T(8,128)S(1)} %get-tuple-element.193, pred[]{:T(512)S(6)} %compare.3), kind=kOutput, calls=%fused_computation.7.clone.1 | convolution fusion | flops 2249036800 | bytes 4003845 | tf_op jit(solution)/shard_map/while/body/eval_jaxpr/dot_general | solution.py:88
  124.2 5.3 %fusion.32 = f32[640,300]{0,1:T(8,128)S(1)} fusion(s32[2560]{0:T(1024)S(1)} %dynamic_slice.25, bf16[384,640]{1,0:T(8,128)(2,1)S(1)} %get-tuple-element.204, bf16[384,20480]{0,1:T(8,128)(2,1)} %get-tuple-element.203, s32[]{:T(128)S(6)} %select_n.27, f32[640,300]{0,1:T(8,128)S(1)} %get-tuple-element.193, pred[]{:T(512)S(6)} %compare.3), kind=kOutput, calls=%fused_computation.7.clone.1 | convolution fusion | flops 2249036800 | bytes 4003845 | tf_op jit(solution)/shard_map/while/body/eval_jaxpr/dot_general | solution.py:88
  129.7 5.3 %fusion.32 = f32[640,300]{0,1:T(8,128)S(1)} fusion(s32[2560]{0:T(1024)S(1)} %dynamic_slice.25, bf16[384,640]{1,0:T(8,128)(2,1)S(1)} %get-tuple-element.204, bf16[384,20480]{0,1:T(8,128)(2,1)} %get-tuple-element.203, s32[]{:T(128)S(6)} %select_n.27, f32[640,300]{0,1:T(8,128)S(1)} %get-tuple-element.193, pred[]{:T(512)S(6)} %compare.3), kind=kOutput, calls=%fused_computation.7.clone.1 | convolution fusion | flops 2249036800 | bytes 4003845 | tf_op jit(solution)/shard_map/while/body/eval_jaxpr/dot_general | solution.py:88
  135.1 5.3 %fusion.32 = f32[640,300]{0,1:T(8,128)S(1)} fusion(s32[2560]{0:T(1024)S(1)} %dynamic_slice.25, bf16[384,640]{1,0:T(8,128)(2,1)S(1)} %get-tuple-element.204, bf16[384,20480]{0,1:T(8,128)(2,1)} %get-tuple-element.203, s32[]{:T(128)S(6)} %select_n.27, f32[640,300]{0,1:T(8,128)S(1)} %get-tuple-element.193, pred[]{:T(512)S(6)} %compare.3), kind=kOutput, calls=%fused_computation.7.clone.1 | convolution fusion | flops 2249036800 | bytes 4003845 | tf_op jit(solution)/shard_map/while/body/eval_jaxpr/dot_general | solution.py:88
  140.6 5.3 %fusion.32 = f32[640,300]{0,1:T(8,128)S(1)} fusion(s32[2560]{0:T(1024)S(1)} %dynamic_slice.25, bf16[384,640]{1,0:T(8,128)(2,1)S(1)} %get-tuple-element.204, bf16[384,20480]{0,1:T(8,128)(2,1)} %get-tuple-element.203, s32[]{:T(128)S(6)} %select_n.27, f32[640,300]{0,1:T(8,128)S(1)} %get-tuple-element.193, pred[]{:T(512)S(6)} %compare.3), kind=kOutput, calls=%fused_computation.7.clone.1 | convolution fusion | flops 2249036800 | bytes 4003845 | tf_op jit(solution)/shard_map/while/body/eval_jaxpr/dot_general | solution.py:88
  146.0 5.3 %fusion.32 = f32[640,300]{0,1:T(8,128)S(1)} fusion(s32[2560]{0:T(1024)S(1)} %dynamic_slice.25, bf16[384,640]{1,0:T(8,128)(2,1)S(1)} %get-tuple-element.204, bf16[384,20480]{0,1:T(8,128)(2,1)} %get-tuple-element.203, s32[]{:T(128)S(6)} %select_n.27, f32[640,300]{0,1:T(8,128)S(1)} %get-tuple-element.193, pred[]{:T(512)S(6)} %compare.3), kind=kOutput, calls=%fused_computation.7.clone.1 | convolution fusion | flops 2249036800 | bytes 4003845 | tf_op jit(solution)/shard_map/while/body/eval_jaxpr/dot_general | solution.py:88
  151.5 5.3 %fusion.32 = f32[640,300]{0,1:T(8,128)S(1)} fusion(s32[2560]{0:T(1024)S(1)} %dynamic_slice.25, bf16[384,640]{1,0:T(8,128)(2,1)S(1)} %get-tuple-element.204, bf16[384,20480]{0,1:T(8,128)(2,1)} %get-tuple-element.203, s32[]{:T(128)S(6)} %select_n.27, f32[640,300]{0,1:T(8,128)S(1)} %get-tuple-element.193, pred[]{:T(512)S(6)} %compare.3), kind=kOutput, calls=%fused_computation.7.clone.1 | convolution fusion | flops 2249036800 | bytes 4003845 | tf_op jit(solution)/shard_map/while/body/eval_jaxpr/dot_general | solution.py:88
  156.9 5.3 %fusion.32 = f32[640,300]{0,1:T(8,128)S(1)} fusion(s32[2560]{0:T(1024)S(1)} %dynamic_slice.25, bf16[384,640]{1,0:T(8,128)(2,1)S(1)} %get-tuple-element.204, bf16[384,20480]{0,1:T(8,128)(2,1)} %get-tuple-element.203, s32[]{:T(128)S(6)} %select_n.27, f32[640,300]{0,1:T(8,128)S(1)} %get-tuple-element.193, pred[]{:T(512)S(6)} %compare.3), kind=kOutput, calls=%fused_computation.7.clone.1 | convolution fusion | flops 2249036800 | bytes 4003845 | tf_op jit(solution)/shard_map/while/body/eval_jaxpr/dot_general | solution.py:88
  163.6 3.5 %all-to-all-start.2 = ((bf16[2,320,300]{1,2,0:T(8,128)(2,1)}), bf16[2,320,300]{1,2,0:T(8,128)(2,1)S(1)}, u32[]{:S(2)}, u32[]{:S(2)}) async-start(bf16[2,320,300]{1,2,0:T(8,128)(2,1)} %copy.25), calls=%async_computation.2 | async-start | bytes 933888 | tf_op jit(solution)/shard_map/all_to_all | solution.py:36
  167.1 7.1 %all-to-all-done.2 = bf16[2,320,300]{1,2,0:T(8,128)(2,1)S(1)} async-done(((bf16[2,320,300]{1,2,0:T(8,128)(2,1)}), bf16[2,320,300]{1,2,0:T(8,128)(2,1)S(1)}, u32[]{:S(2)}, u32[]{:S(2)}) %all-to-all-start.2) | async-done | bytes 384032 | tf_op jit(solution)/shard_map/all_to_all | solution.py:36
  175.1 13.4 %psum.35 = f32[300,7]{0,1:T(8,128)S(1)} all-reduce(f32[300,7]{0,1:T(8,128)S(1)} %convolution_bitcast_fusion), channel_id=1, replica_groups=mesh['genes_0'=4,'genes_1'=4,'genes_2'=2,'genes_3'=2,'cols'=2] {'genes_0'}, use_global_device_ids=true, to_apply=%region_8.9 | all-reduce | flops 2100 | bytes 16800 | tf_op jit(solution)/shard_map/psum | solution.py:42
  188.5 11.1 %psum.36 = f32[300,7]{0,1:T(8,128)S(1)} all-reduce(f32[300,7]{0,1:T(8,128)S(1)} %psum.35), channel_id=1, replica_groups=mesh['genes_0'=4,'genes_1'=4,'genes_2'=2,'genes_3'=2,'cols'=2] {'genes_1'}, use_global_device_ids=true, to_apply=%region_9.10 | all-reduce | flops 2100 | bytes 16800 | tf_op jit(solution)/shard_map/psum | solution.py:42
  199.6 7.3 %psum.37 = f32[300,7]{0,1:T(8,128)S(1)} all-reduce(f32[300,7]{0,1:T(8,128)S(1)} %psum.36), channel_id=1, replica_groups=mesh['genes_0'=4,'genes_1'=4,'genes_2'=2,'genes_3'=2,'cols'=2] {'genes_2'}, use_global_device_ids=true, to_apply=%region_10.11 | all-reduce | flops 2100 | bytes 16800 | tf_op jit(solution)/shard_map/psum | solution.py:42
  206.8 13.5 %psum.38 = f32[300,7]{0,1:T(8,128)S(1)} all-reduce(f32[300,7]{0,1:T(8,128)S(1)} %psum.37), channel_id=1, replica_groups=mesh['genes_0'=4,'genes_1'=4,'genes_2'=2,'genes_3'=2,'cols'=2] {'genes_3'}, use_global_device_ids=true, to_apply=%region_11.12 | all-reduce | flops 2100 | bytes 16800 | tf_op jit(solution)/shard_map/psum | solution.py:42
  220.3 5.0 %psum.39 = f32[300,7]{0,1:T(8,128)S(1)} all-reduce(f32[300,7]{0,1:T(8,128)S(1)} %psum.38), channel_id=1, replica_groups=mesh['genes_0'=4,'genes_1'=4,'genes_2'=2,'genes_3'=2,'cols'=2] {'cols'}, use_global_device_ids=true, to_apply=%region_12.13 | all-reduce | flops 2100 | bytes 16800 | tf_op jit(solution)/shard_map/psum | solution.py:42
  (48 shorter events, 6.2 us)
Async XLA Ops:
  7.2 6.0 %copy-start = (s32[320,300]{0,1:T(8,128)S(1)}, s32[320,300]{0,1:T(8,128)}, u32[]{:S(2)}) copy-start(s32[320,300]{0,1:T(8,128)} %param.8) | copy-start | bytes 1152004
  7.2 111.5 %all-gather.2.cloned.1.call-start = ((), (), s32[]{:S(2)}) async-start(), calls=%async_computation.3 | async-start | bytes 15974400 | tf_op jit(solution)/shard_map/all_gather | solution.py:115
  37.0 10.7 %all-to-all-start = ((bf16[2,384,320]{1,2,0:T(8,128)(2,1)}), bf16[2,384,320]{1,2,0:T(8,128)(2,1)S(1)}, u32[]{:S(2)}, u32[]{:S(2)}) async-start(bf16[2,384,320]{1,2,0:T(8,128)(2,1)} %broadcast_in_dim.34), calls=%async_computation | async-start | bytes 983040 | tf_op jit(solution)/shard_map/all_to_all | solution.py:22
  118.7 48.4 %copy-start.2 = (f32[320]{0:T(512)S(1)}, f32[320]{0:T(512)}, u32[]{:S(2)}) copy-start(f32[320]{0:T(512)} %param.9) | copy-start | bytes 3844
  163.6 10.6 %all-to-all-start.2 = ((bf16[2,320,300]{1,2,0:T(8,128)(2,1)}), bf16[2,320,300]{1,2,0:T(8,128)(2,1)S(1)}, u32[]{:S(2)}, u32[]{:S(2)}) async-start(bf16[2,320,300]{1,2,0:T(8,128)(2,1)} %copy.25), calls=%async_computation.2 | async-start | bytes 933888 | tf_op jit(solution)/shard_map/all_to_all | solution.py:36
  174.5 51.5 %copy-start.1 = (f32[320,300]{0,1:T(8,128)}, f32[320,300]{0,1:T(8,128)S(1)}, u32[]{:S(2)}) copy-start(f32[320,300]{0,1:T(8,128)S(1)} %get-tuple-element.136) | copy-start | bytes 1152004
Sparse Core Ops, SparseCore 0:
  13.3 105.3 all-gather.1
where the time goes:
time: 234 us; the launch traced here: 233 us
  waiting for transfers between devices  84.7 us (36%)
  blocking collectives  72.1 us (31%)
  matrix products  43.2 us (18%)
  between operations  14.2 us (6%)
  local copies, waits for them, and re-layouts  7.35 us (3%)
  starting transfers between devices  7 us (3%)
  other arithmetic  4.01 us (2%)
    all_gather x1, waiting for transfers between devices, local(): lax.all_gather(scaled, GENES, axis=1, tiled=True)  70.7 us
    psum x5, blocking collectives, one_axis_at_a_time(): x = lax.psum(x, axis)  50.2 us
    dot_general x8, matrix products, tile_term(): return jnp.dot(adjacency, member_block, preferred_element_type=jnp.float32)  42.8 us
    all_to_all x1, blocking collectives, sent_to_all(): return lax.all_to_all(copies, axis, split_axis=0, concat_axis=0, tiled=True)  22 us
    all_to_all x1, waiting for transfers between devices, sum_at_owner(): blocks = lax.all_to_all(split_up(x, dim, count), axis, 0, 0, tiled=True)  7.13 us
    all_to_all x1, waiting for transfers between devices, sent_to_all(): return lax.all_to_all(copies, axis, split_axis=0, concat_axis=0, tiled=True)  6.84 us
  transfers between devices with their start and end apart: 3, of which 3 were waited for; matrix products, arithmetic and copies ran while one was open for 1% of the time, Pallas kernels for 0%

commit v1 on v0

v1 whole, which is shorter than its diff:
```python
import functools

import jax
import jax.numpy as jnp
from jax import lax
from jax.experimental import pallas as pl
from jax.experimental.pallas import tpu as pltpu
from jax.sharding import Mesh
from jax.sharding import PartitionSpec as P

G = 40960
SAMPLES = 384
K = 300
KP = 304
OWN = 320
HALF = OWN // 2
LINE = 4
CHUNK = 2 * OWN
STEP = 2 * LINE * HALF
ROWS = LINE * CHUNK
COLS = LINE * STEP
TILE = 512
TILES = ROWS // TILE
KEEP = 384
AXES = ("z", "y", "xh", "c", "xl")
OFFSETS = (0, 1, 3, 2)
SEEN_AS = (0, 2, 1, 3)
NT = (((1,), (1,)), ((), ()))


def kernel(
    depth, compact, resample, expression, labels, ref_kim, conn_out, pres_out,
    rows, cols, lt, adj, acc, pair, sent, got, own_ids, member, sums_xc, sums_y, sums_z,
    send_rows, recv_rows, send_fwd, recv_fwd, send_near, recv_near, send_far, recv_far,
    send_pair, recv_pair, send_sum, recv_sum, send_xc, recv_xc, send_yz, recv_yz,
):
    f32, bf16 = jnp.float32, jnp.bfloat16
    z, y, core = lax.axis_index("z"), lax.axis_index("y"), lax.axis_index("c")
    x = lax.axis_index("xh") * 2 + lax.axis_index("xl")
    other = 1 - core

    def at_x(place, c=None):
        there = lax.rem(x + OFFSETS[place], LINE)
        device = {"xh": there // 2, "xl": lax.rem(there, 2)}
        if c is not None:
            device["c"] = c
        return device

    def at_y(place):
        return {"y": lax.rem(y + OFFSETS[place], LINE)}

    def at_z(place):
        return {"z": lax.rem(z + OFFSETS[place], LINE)}

    partner = {"c": other}

    barrier = pltpu.get_barrier_semaphore()
    peers = [partner]
    for place in range(1, LINE):
        peers += [at_x(place), at_x(place, other), at_y(place), at_z(place)]
    for peer in peers:
        pl.semaphore_signal(barrier, inc=1, device_id=peer, device_id_type=pl.DeviceIdType.MESH)

    def remote(src, dst, send_sem, recv_sem, device):
        return pltpu.make_async_remote_copy(
            src_ref=src, dst_ref=dst, send_sem=send_sem, recv_sem=recv_sem,
            device_id=device, device_id_type=pl.DeviceIdType.MESH,
        )

    started = []

    def send(*args):
        copy = remote(*args)
        copy.start()
        started.append(copy)

    drawn = resample[...]
    ones_at = lax.broadcasted_iota(jnp.int32, (SAMPLES, SAMPLES), 0) == drawn
    hits = jnp.where(ones_at, 1.0, 0.0)
    times = jnp.sum(hits, axis=1, keepdims=True)
    if compact:
        times_row = lax.dot_general(
            jnp.ones((16, SAMPLES), bf16), hits.astype(bf16), NT, preferred_element_type=f32
        )
        present = jnp.where(times_row > 0.5, 1.0, 0.0)
        before = jnp.where(
            lax.broadcasted_iota(jnp.int32, (SAMPLES, SAMPLES), 0)
            < lax.broadcasted_iota(jnp.int32, (SAMPLES, SAMPLES), 1),
            1.0,
            0.0,
        ).astype(bf16)
        rank = jnp.dot(present.astype(bf16), before, preferred_element_type=f32)
        rank = jnp.where(present > 0.5, rank, -1.0)[0:1, :]
        place_of = rank.astype(jnp.int32)
    else:
        place_of = lax.broadcasted_iota(jnp.int32, (1, SAMPLES), 1)
    pick = jnp.where(
        lax.broadcasted_iota(jnp.int32, (depth, SAMPLES), 0) == place_of, 1.0, 0.0
    ).astype(bf16)
    values = expression[...]
    mean = jnp.sum(values * times, axis=0, keepdims=True) * (1.0 / SAMPLES)
    centered = values - mean
    total = jnp.sum(centered * centered * times, axis=0, keepdims=True)
    scaled = (centered * lax.rsqrt(total + 1e-06)).astype(bf16)
    weighted = (scaled.astype(f32) * times).astype(bf16)
    over_samples = (((0,), (1,)), ((), ()))
    side = lax.dot_general(weighted, pick, over_samples, preferred_element_type=f32)
    front = lax.dot_general(scaled, pick, over_samples, preferred_element_type=f32)
    marks = labels[...].astype(f32)
    module = lax.broadcasted_iota(jnp.int32, (OWN, K), 1).astype(f32) - 150.0
    id_column = jnp.sum(marks * module, axis=1, keepdims=True)
    lane = lax.broadcasted_iota(jnp.int32, (OWN, depth), 1)
    front = jnp.where(lane == depth - 1, id_column, front).astype(bf16)
    rows[pl.ds(pl.multiple_of(core * OWN, OWN), OWN), :] = side.astype(bf16)
    cols[0:HALF, :] = front[0:HALF]
    cols[STEP // 2 : STEP // 2 + HALF, :] = front[HALF:OWN]

    pl.semaphore_wait(barrier, len(peers))

    def row_block(chunk, c):
        return rows.at[pl.ds(pl.multiple_of(chunk * CHUNK + c * OWN, OWN), OWN), :]

    def col_block(step, part, slot):
        return cols.at[pl.ds(step * STEP + part * (STEP // 2) + slot * HALF, HALF), :]

    def near_index(part, place):
        return part * LINE + place

    def far_index(part, step, slot):
        return (part * LINE + step) * LINE + slot

    along = (at_z, at_y)
    across = (at_y, at_z)
    for place in range(1, LINE):
        for part in range(2):
            send(
                col_block(0, part, 0), col_block(0, part, SEEN_AS[place]),
                send_near.at[near_index(part, place)],
                recv_near.at[near_index(part, SEEN_AS[place])], along[part](place),
            )
        send(
            row_block(0, core), row_block(SEEN_AS[place], core),
            send_rows.at[place], recv_rows.at[SEEN_AS[place]], at_x(place),
        )
        if place == 1:
            send(row_block(0, core), row_block(0, core), send_fwd.at[0], recv_fwd.at[0], partner)

    def forward_columns(part, slot):
        for place in range(1, LINE):
            send(
                col_block(0, part, slot), col_block(SEEN_AS[place], part, slot),
                send_far.at[far_index(part, place, slot)],
                recv_far.at[far_index(part, SEEN_AS[place], slot)], across[part](place),
            )

    def wait_near(part, place):
        block = col_block(0, part, place)
        remote(
            block, block, send_near.at[near_index(part, place)],
            recv_near.at[near_index(part, place)], along[part](place),
        ).wait_recv()

    def wait_far(step):
        for part in range(2):
            for slot in range(LINE):
                block = col_block(step, part, slot)
                remote(
                    block, block, send_far.at[far_index(part, step, slot)],
                    recv_far.at[far_index(part, step, slot)], across[part](step),
                ).wait_recv()

    def pass_rows(chunk):
        block = row_block(chunk, core)
        remote(block, block, send_rows.at[chunk], recv_rows.at[chunk], at_x(chunk)).wait_recv()
        copy = remote(block, block, send_fwd.at[chunk], recv_fwd.at[chunk], partner)
        copy.start()

    def wait_rows(chunk):
        block = row_block(chunk, other)
        remote(block, block, send_fwd.at[chunk], recv_fwd.at[chunk], partner).wait_recv()

    for part in range(2):
        forward_columns(part, 0)

    acc[...] = jnp.zeros_like(acc)
    reach = lax.broadcasted_iota(jnp.int32, (16, K), 1).astype(f32) - 150.0
    own_ids[:, 0:OWN] = lax.dot_general(
        reach.astype(bf16), marks.astype(bf16), NT, preferred_element_type=f32
    )
    member[...] = jnp.where(
        lax.broadcasted_iota(jnp.int32, (OWN, KEEP), 1).astype(f32) - 150.0 == id_column, 1.0, 0.0
    )

    for place in range(1, LINE):
        for part in range(2):
            wait_near(part, place)
            forward_columns(part, place)
        if place < 3:
            pass_rows(place)
    wait_rows(0)

    def pair_slice(chunk, c):
        return acc.at[:, pl.ds(pl.multiple_of(chunk * CHUNK + c * 256, 128), KEEP)]

    def to_partner(chunk):
        return remote(
            pair_slice(chunk, other), pair.at[chunk], send_pair.at[chunk], recv_pair.at[chunk],
            partner,
        )

    def to_owner(chunk):
        return remote(
            sent.at[chunk], got.at[SEEN_AS[chunk]], send_sum.at[chunk],
            recv_sum.at[SEEN_AS[chunk]], at_x(chunk),
        )

    def pass_sum(chunk):
        to_partner(chunk).wait_recv()
        mine = acc[:, pl.ds(pl.multiple_of(chunk * CHUNK + core * 256, 128), KEEP)]
        sent[chunk] = (mine + pair[chunk]).astype(bf16)
        to_owner(chunk).start()

    def one_tile(t, carry):
        step, turn = t // TILES, lax.rem(t, TILES)
        tile = jnp.where(step == LINE - 1, TILES - 1 - turn, turn)
        base = pl.multiple_of(step * STEP, STEP)
        side_at = pl.multiple_of(tile * TILE, TILE)

        @pl.when(t == 1)
        def _():
            wait_rows(1)

        @pl.when(t == 2)
        def _():
            pass_rows(3)
            wait_rows(2)

        @pl.when(t == 3)
        def _():
            wait_rows(3)

        for far in range(1, LINE):

            @pl.when(t == far * TILES)
            def _():
                wait_far(far)

        @pl.when(turn == 0)
        def _():
            last = lax.broadcasted_iota(jnp.int32, (16, depth), 1) == depth - 1
            ids = lax.dot_general(
                jnp.where(last, 1.0, 0.0).astype(bf16), cols[pl.ds(base, STEP), :], NT,
                preferred_element_type=f32,
            )
            which = lax.broadcasted_iota(jnp.int32, (KP, STEP), 0).astype(f32) - 150.0
            lt[...] = jnp.where(which == ids[0:1, :], 1.0, 0.0).astype(bf16)

        side_block = rows[pl.ds(side_at, TILE), :]
        for part in range(STEP // 256):
            scores = lax.dot_general(
                cols[pl.ds(base + part * 256, 256), :], side_block, NT, preferred_element_type=f32
            )
            squares = scores * scores
            adj[part * 256 : (part + 1) * 256, :] = (squares * squares * squares).astype(bf16)
        acc[:, pl.ds(side_at, TILE)] += jnp.dot(lt[...], adj[...], preferred_element_type=f32)

        ends = (LINE - 1) * TILES
        for after in range(1, TILES):

            @pl.when(t == ends + after)
            def _():
                to_partner(LINE - after).start()
                if after > 1:
                    pass_sum(LINE - after + 1)

        return carry

    lax.fori_loop(0, LINE * TILES, one_tile, 0)

    to_partner(0).wait_recv()
    conn = acc[:, pl.ds(pl.multiple_of(core * 256, 128), KEEP)] + pair[0]
    for chunk in range(1, LINE):
        remote(
            sent.at[chunk], got.at[chunk], send_sum.at[chunk], recv_sum.at[chunk], at_x(chunk)
        ).wait_recv()
        conn = conn + got[chunk].astype(f32)
    conn = jnp.where(core == 0, conn, pltpu.roll(conn, KEEP - 64, 1))

    which = lax.broadcasted_iota(jnp.int32, (KP, OWN), 0).astype(f32) - 150.0
    valid = conn[:, 0:OWN]
    kim = jnp.sum(jnp.where(which == own_ids[0:1, 0:OWN], valid, 0.0), axis=0, keepdims=True)
    rowsum = jnp.sum(valid, axis=0, keepdims=True)
    ref = ref_kim[...]
    stacked = jnp.concatenate(
        [kim, kim * kim, ref, ref * ref, kim * ref, rowsum, jnp.ones_like(kim), jnp.zeros_like(kim)],
        axis=0,
    )
    sums = jnp.dot(
        stacked, member[...], precision=lax.Precision.HIGHEST, preferred_element_type=f32
    )

    def wait_sent(copies):
        for copy in copies:
            copy.wait_send()

    place_xc = x * 2 + core
    sums_xc[place_xc] = sums
    copies = []
    for place in range(LINE):
        for flip in range(2):
            if place == 0 and flip == 0:
                continue
            peer = at_x(place, core if flip == 0 else other)
            copies.append((
                remote(
                    sums_xc.at[place_xc], sums_xc.at[place_xc], send_xc.at[place * 2 + flip],
                    recv_xc.at[SEEN_AS[place] * 2 + flip], peer,
                ),
                place, flip,
            ))
    for copy, _, _ in copies:
        copy.start()

    conn_out[...] = conn.T[0:OWN, 0:K]

    for copy, place, flip in copies:
        there = lax.rem(x + OFFSETS[place], LINE) * 2 + (core if flip == 0 else other)
        remote(
            sums_xc.at[there], sums_xc.at[there], send_xc.at[place * 2 + flip],
            recv_xc.at[place * 2 + flip], partner,
        ).wait_recv()
    total_sums = sums_xc[0]
    for index in range(1, 2 * LINE):
        total_sums = total_sums + sums_xc[index]
    wait_sent([copy for copy, _, _ in copies])

    for axis, (mine, buffer, at) in enumerate(((y, sums_y, at_y), (z, sums_z, at_z))):
        buffer[mine] = total_sums
        copies = []
        for place in range(1, LINE):
            copy = remote(
                buffer.at[mine], buffer.at[mine], send_yz.at[axis * LINE + place],
                recv_yz.at[axis * LINE + SEEN_AS[place]], at(place),
            )
            copy.start()
            copies.append(copy)
        for place in range(1, LINE):
            there = lax.rem(mine + OFFSETS[place], LINE)
            remote(
                buffer.at[there], buffer.at[there], send_yz.at[axis * LINE + place],
                recv_yz.at[axis * LINE + place], at(place),
            ).wait_recv()
        total_sums = buffer[0]
        for index in range(1, LINE):
            total_sums = total_sums + buffer[index]
        wait_sent(copies)

    s_k, s_kk, s_y, s_yy, s_ky, s_r, n = (total_sums[i : i + 1, 0:K] for i in range(7))
    mean_x = s_k / (n * n)
    var_x = jnp.maximum(s_kk / (n * n * n) - mean_x * mean_x, 0.0001)
    mean_y = s_y / n
    var_y = jnp.maximum(s_yy / n - mean_y * mean_y, 0.01)
    cross = s_ky / (n * n) - mean_x * mean_y
    between = (s_r - s_k) / (n * (float(G) - n))
    pres_out[0:1, :] = (mean_x - between) * jnp.sqrt(n / var_x)
    pres_out[1:2, :] = cross * jnp.sqrt(n / (var_x * var_y))

    wait_sent(started)
    for chunk in range(1, LINE):
        block = row_block(chunk, core)
        remote(block, block, send_fwd.at[chunk], recv_fwd.at[chunk], partner).wait_send()
        to_owner(chunk).wait_send()
    for chunk in range(LINE):
        to_partner(chunk).wait_send()


def whole(depth, compact, collective, resample, expression, labels, ref_kim):
    f32, bf16 = jnp.float32, jnp.bfloat16
    dma = pltpu.SemaphoreType.DMA
    vmem = pl.BlockSpec(memory_space=pltpu.VMEM)
    scratch = [
        pltpu.VMEM((ROWS, depth), bf16),
        pltpu.VMEM((COLS, depth), bf16),
        pltpu.VMEM((KP, STEP), bf16),
        pltpu.VMEM((STEP, TILE), bf16),
        pltpu.VMEM((KP, ROWS), f32),
        pltpu.VMEM((LINE, KP, KEEP), f32),
        pltpu.VMEM((LINE, KP, KEEP), bf16),
        pltpu.VMEM((LINE, KP, KEEP), bf16),
        pltpu.VMEM((16, KEEP), f32),
        pltpu.VMEM((OWN, KEEP), f32),
        pltpu.VMEM((2 * LINE, 8, KEEP), f32),
        pltpu.VMEM((LINE, 8, KEEP), f32),
        pltpu.VMEM((LINE, 8, KEEP), f32),
    ]
    for count in (LINE, LINE, 2 * LINE, 2 * LINE * LINE, LINE, LINE, 2 * LINE, 2 * LINE):
        scratch += [dma((count,)), dma((count,))]
    return pl.pallas_call(
        functools.partial(kernel, depth, compact),
        out_shape=(
            jax.ShapeDtypeStruct((OWN, K), f32),
            jax.ShapeDtypeStruct((2, K), f32),
        ),
        in_specs=[vmem] * 4,
        out_specs=(vmem, vmem),
        scratch_shapes=scratch,
        compiler_params=pltpu.CompilerParams(
            collective_id=collective, has_side_effects=True, vmem_limit_bytes=60 * 1024 * 1024
        ),
        name=f"network_{depth}",
    )(resample, expression, labels, ref_kim)


def local(expression, resample, labels, ref_kim):
    samples = jnp.arange(SAMPLES, dtype=jnp.int32)
    distinct = jnp.sum(jnp.any(resample[:, None] == samples[None, :], axis=0).astype(jnp.int32))
    return lax.cond(
        distinct <= 255,
        functools.partial(whole, 256, True, 0),
        functools.partial(whole, 512, False, 1),
        resample.reshape(1, SAMPLES),
        expression,
        labels,
        ref_kim.reshape(1, OWN),
    )


def solution(mesh):
    torus = Mesh(mesh.devices.reshape(4, 4, 2, 2, 2), AXES)
    placed = (P(None, AXES), P(), P(AXES, None), P(AXES))
    return jax.shard_map(
        local, mesh=torus, in_specs=placed, out_specs=(P(AXES, None), P()), check_vma=False
    )
```

time: 234 us -> 78.1 us (0.33)
  waiting for transfers between devices: 84.7 us -> 0 us
  blocking collectives: 72.1 us -> 0 us
  Pallas kernels: 0 us -> 68 us
  matrix products: 43.2 us -> 0 us
  between operations: 14.2 us -> 1.32 us
  starting transfers between devices: 7 us -> 0 us
  other arithmetic: 4.01 us -> 1.48 us
    all_gather x1 -> x0, waiting for transfers between devices: 70.7 us -> none  [local(): lax.all_gather(scaled, GENES, axis=1, tiled=True)]
    pallas_call x0 -> x1, Pallas kernels: none -> 68 us  [whole(): pl.pallas_call(functools.partial(kernel, depth, compact), out_shape=(jax....]
    psum x5 -> x0, blocking collectives: 50.2 us -> none  [one_axis_at_a_time(): x = lax.psum(x, axis)]
    dot_general x9 -> x0, matrix products: 43.2 us -> none  [the longest x8 42.8 us: tile_term(): return jnp.dot(adjacency, member_block, preferred_element_type=jnp.float32)]
    all_to_all x1 -> x0, blocking collectives: 22 us -> none  [sent_to_all(): return lax.all_to_all(copies, axis, split_axis=0, concat_axis=0, tiled=True)]
    all_to_all x2 -> x0, waiting for transfers between devices: 14 us -> none  [the longest x1 7.13 us: sum_at_owner(): blocks = lax.all_to_all(split_up(x, dim, count), axis, 0, 0, tiled=True)]
    all_to_all x2 -> x0, starting transfers between devices: 6.96 us -> none  [the longest x1 3.48 us: sent_to_all(): return lax.all_to_all(copies, axis, split_axis=0, concat_axis=0, tiled=True)]
    another operation x7 -> x2, local copies, waits for them, and re-layouts: 0.05 us -> 3.09 us  [local_sums(): jnp.stack([kim, kim * kim, ref_kim, ref_kim * ref_kim, kim * ref_kim, row...]
  transfers between devices with their start and end apart: 3 -> 0, of which waited for: 3 -> 0; matrix products, arithmetic and copies ran while one was open for 1% -> 0% of each run, Pallas kernels for 0% -> 0%
where the time goes in v1:
time: 78.1 us; the launch traced here: 77.1 us
  Pallas kernels  68 us (87%)
  local copies, waits for them, and re-layouts  6.25 us (8%)
  other arithmetic  1.48 us (2%)
  between operations  1.32 us (2%)
    pallas_call x1, Pallas kernels, whole(): pl.pallas_call(functools.partial(kernel, depth, compact), out_shape=(jax....  68 us
    another operation x2, local copies, waits for them, and re-layouts  3.09 us

profile of v1, /device:TPU:1, one launch (start us, length us, event | category | flops | bytes accessed | tf_op | source)
XLA Modules:
  0.0 77.1 jit_solution(1553035746979098407)
XLA Ops:
  0.6 0.0 copy-start.4
  0.6 0.8 %fusion = pred[384]{0:T(512)(128)(4,1)S(1)} fusion(s32[384]{0:T(512)} %param.7), kind=kLoop, calls=%fused_computation.1 | loop fusion | flops 294528 | bytes 1920 | tf_op jit(solution)/shard_map/reduce_or | solution.py:416
  1.5 0.0 copy-start.3
  1.5 0.6 convert_reduce_fusion
  2.8 0.0 copy-done.4
  2.8 0.0 copy-done.3
  2.8 73.5 %conditional.1 = (f32[2,300]{1,0:T(2,128)S(1)}, f32[320,300]{0,1:T(8,128)S(1)}) conditional(s32[]{:T(128)} %convert_element_type.7, (s32[384]{0:T(512)S(1)}, f32[384,320]{0,1:T(8,128)}, s32[320,300]{0,1:T(8,128)}, f32[320]{0:T(512)S(1)}) %tuple.32, (s32[384]{0:T(512)S(1)}, f32[384,320]{0,1:T(8,128)}, s32[320,300]{0,1:T(8,128)}, ...), branch_computations={%region_2.0_spmd, %region_3.0_spmd} | conditional | bytes 4490796 | solution.py:417
  2.8 0.0 copy-start.1
  2.8 0.6 reshape.16.ref_kim
  3.4 0.6 reshape.14.resample
  4.0 2.0 %copy.24.labels = s32[320,300]{1,0:T(8,128)} copy(s32[320,300]{0,1:T(8,128)} %get-tuple-element.64) | data formatting | bytes 768000 | tf_op jit(solution)/shard_map
  6.0 0.0 copy-done.1
  6.0 1.1 %copy.23.expression = f32[384,320]{1,0:T(8,128)} copy(f32[384,320]{0,1:T(8,128)S(1)} %copy-done.1) | data formatting | bytes 983040 | tf_op jit(solution)/shard_map
  7.1 68.0 %network_256.1 = (f32[320,300]{1,0:T(8,128)}, f32[2,300]{1,0:T(2,128)S(1)}) custom-call(s32[1,384]{1,0:T(1,128)} %reshape.14.resample, f32[384,320]{1,0:T(8,128)} %copy.23.expression, s32[320,300]{1,0:T(8,128)} %copy.24.labels, f32[1,320]{1,0:T(1,128)} %reshape.16.ref_kim), custom_call_target="tpu_custom_call" | custom-call | tf_op jit(solution)/shard_map/cond/branch_1_fun/network_256/pallas_call | solution.py:398
  75.1 1.2 %copy.27 = f32[320,300]{0,1:T(8,128)S(1)} copy(f32[320,300]{1,0:T(8,128)} %get-tuple-element.70) | data formatting | bytes 768000 | tf_op jit(solution)/shard_map/cond | solution.py:417
  76.3 0.0 copy-start.2
  76.3 0.6 copy.33
  76.9 0.2 copy-done.2
Async XLA Ops:
  0.6 2.2 %copy-start.4 = (f32[320]{0:T(512)S(1)}, f32[320]{0:T(512)}, u32[]{:S(2)}) copy-start(f32[320]{0:T(512)} %param.9) | copy-start | bytes 3844
  1.5 1.3 %copy-start.3 = (s32[384]{0:T(512)S(1)}, s32[384]{0:T(512)}, u32[]{:S(2)}) copy-start(s32[384]{0:T(512)} %param.7) | copy-start | bytes 4612
  2.8 3.2 %copy-start.1 = (f32[384,320]{0,1:T(8,128)S(1)}, f32[384,320]{0,1:T(8,128)}, u32[]{:S(2)}) copy-start(f32[384,320]{0,1:T(8,128)} %get-tuple-element.63) | copy-start | bytes 1474564 | tf_op jit(solution)/shard_map/cond
  76.3 0.8 %copy-start.2 = (f32[320,300]{0,1:T(8,128)}, f32[320,300]{0,1:T(8,128)S(1)}, u32[]{:S(2)}) copy-start(f32[320,300]{0,1:T(8,128)S(1)} %get-tuple-element.79) | copy-start | bytes 1152004

commit v2 on v1

--- a/solution.py
+++ b/solution.py
@@ -29,10 +29,12 @@
 
 
 def kernel(
-    depth, compact, resample, expression, labels, ref_kim, conn_out, pres_out,
-    rows, cols, lt, adj, acc, pair, sent, got, own_ids, member, sums_xc, sums_y, sums_z,
+    depth, compact, resample, expression, labels, ref_kim, conn_out, pres_out, count_out,
+    rows, cols, lt, adj, acc, pair, sent, got, info, side_ids, side_lt, kim_rows, parts, stats,
+    sums_y, sums_z,
     send_rows, recv_rows, send_fwd, recv_fwd, send_near, recv_near, send_far, recv_far,
-    send_pair, recv_pair, send_sum, recv_sum, send_xc, recv_xc, send_yz, recv_yz,
+    send_pair, recv_pair, send_sum, recv_sum, send_info, recv_info, send_part, recv_part,
+    send_yz, recv_yz,
 ):
     f32, bf16 = jnp.float32, jnp.bfloat16
     z, y, core = lax.axis_index("z"), lax.axis_index("y"), lax.axis_index("c")
@@ -74,46 +76,50 @@
         copy.start()
         started.append(copy)
 
-    drawn = resample[...]
-    ones_at = lax.broadcasted_iota(jnp.int32, (SAMPLES, SAMPLES), 0) == drawn
-    hits = jnp.where(ones_at, 1.0, 0.0)
-    times = jnp.sum(hits, axis=1, keepdims=True)
+    sample = lax.broadcasted_iota(jnp.int32, (SAMPLES, SAMPLES), 0)
+    hits = jnp.where(sample == resample[...], 1.0, 0.0).astype(bf16)
+    times = lax.dot_general(
+        jnp.ones((16, SAMPLES), bf16), hits, NT, preferred_element_type=f32
+    )
+    present = jnp.where(times > 0.5, 1.0, 0.0)
     if compact:
-        times_row = lax.dot_general(
-            jnp.ones((16, SAMPLES), bf16), hits.astype(bf16), NT, preferred_element_type=f32
-        )
-        present = jnp.where(times_row > 0.5, 1.0, 0.0)
         before = jnp.where(
-            lax.broadcasted_iota(jnp.int32, (SAMPLES, SAMPLES), 0)
-            < lax.broadcasted_iota(jnp.int32, (SAMPLES, SAMPLES), 1),
-            1.0,
-            0.0,
+            sample < lax.broadcasted_iota(jnp.int32, (SAMPLES, SAMPLES), 1), 1.0, 0.0
         ).astype(bf16)
         rank = jnp.dot(present.astype(bf16), before, preferred_element_type=f32)
-        rank = jnp.where(present > 0.5, rank, -1.0)[0:1, :]
-        place_of = rank.astype(jnp.int32)
+        place_of = jnp.where(present > 0.5, rank, -1.0)[0:1, :].astype(jnp.int32)
     else:
         place_of = lax.broadcasted_iota(jnp.int32, (1, SAMPLES), 1)
+    count_out[0] = jnp.sum(present[0:1, :].astype(jnp.int32))
+    times = times[0:1, :]
     pick = jnp.where(
         lax.broadcasted_iota(jnp.int32, (depth, SAMPLES), 0) == place_of, 1.0, 0.0
     ).astype(bf16)
     values = expression[...]
-    mean = jnp.sum(values * times, axis=0, keepdims=True) * (1.0 / SAMPLES)
+    mean = jnp.sum(values * times, axis=1, keepdims=True) * (1.0 / SAMPLES)
     centered = values - mean
-    total = jnp.sum(centered * centered * times, axis=0, keepdims=True)
+    total = jnp.sum(centered * centered * times, axis=1, keepdims=True)
     scaled = (centered * lax.rsqrt(total + 1e-06)).astype(bf16)
     weighted = (scaled.astype(f32) * times).astype(bf16)
-    over_samples = (((0,), (1,)), ((), ()))
-    side = lax.dot_general(weighted, pick, over_samples, preferred_element_type=f32)
-    front = lax.dot_general(scaled, pick, over_samples, preferred_element_type=f32)
+    side = lax.dot_general(weighted, pick, NT, preferred_element_type=f32)
+    front = lax.dot_general(scaled, pick, NT, preferred_element_type=f32)
     marks = labels[...].astype(f32)
-    module = lax.broadcasted_iota(jnp.int32, (OWN, K), 1).astype(f32) - 150.0
-    id_column = jnp.sum(marks * module, axis=1, keepdims=True)
-    lane = lax.broadcasted_iota(jnp.int32, (OWN, depth), 1)
-    front = jnp.where(lane == depth - 1, id_column, front).astype(bf16)
+    module = lax.broadcasted_iota(jnp.int32, (K, depth), 0).astype(f32) - 150.0
+    module = jnp.where(lax.broadcasted_iota(jnp.int32, (K, depth), 1) == depth - 1, module, 0.0)
+    front = front + lax.dot_general(
+        marks.astype(bf16), module.astype(bf16), (((0,), (0,)), ((), ())),
+        preferred_element_type=f32,
+    )
+    front = front.astype(bf16)
     rows[pl.ds(pl.multiple_of(core * OWN, OWN), OWN), :] = side.astype(bf16)
     cols[0:HALF, :] = front[0:HALF]
     cols[STEP // 2 : STEP // 2 + HALF, :] = front[HALF:OWN]
+    place_xc = x * 2 + core
+    module = lax.broadcasted_iota(jnp.int32, (K, OWN), 0).astype(f32) - 150.0
+    info[place_xc, 0:1, :] = jnp.full((1, KEEP), -1000.0, f32)
+    info[place_xc, 1:2, :] = jnp.zeros((1, KEEP), f32)
+    info[place_xc, 0:1, 0:OWN] = jnp.sum(marks * module, axis=0, keepdims=True)
+    info[place_xc, 1:2, 0:OWN] = ref_kim[...]
 
     pl.semaphore_wait(barrier, len(peers))
 
@@ -131,6 +137,39 @@
 
     along = (at_z, at_y)
     across = (at_y, at_z)
+
+    def group(place, flip):
+        if place == 0:
+            return partner
+        return at_x(place) if flip == 0 else at_x(place, other)
+
+    mates = [(0, 1)] + [(place, flip) for place in range(1, LINE) for flip in range(2)]
+
+    def to_mates(buffer, send_sem, recv_sem):
+        for place, flip in mates:
+            send(
+                buffer.at[place_xc], buffer.at[place_xc], send_sem.at[place * 2 + flip],
+                recv_sem.at[SEEN_AS[place] * 2 + flip], group(place, flip),
+            )
+
+    def from_mates(buffer, send_sem, recv_sem):
+        for place, flip in mates:
+            there = lax.rem(x + OFFSETS[place], LINE) * 2 + (core if flip == 0 else other)
+            remote(
+                buffer.at[there], buffer.at[there], send_sem.at[place * 2 + flip],
+                recv_sem.at[place * 2 + flip], group(place, flip),
+            ).wait_recv()
+
+    def forward_columns(part, slot, places):
+        for place in places:
+            send(
+                col_block(0, part, slot), col_block(SEEN_AS[place], part, slot),
+                send_far.at[far_index(part, place, slot)],
+                recv_far.at[far_index(part, SEEN_AS[place], slot)], across[part](place),
+            )
+
+    to_mates(info, send_info, recv_info)
+    send(row_block(0, core), row_block(0, core), send_fwd.at[0], recv_fwd.at[0], partner)
     for place in range(1, LINE):
         for part in range(2):
             send(
@@ -142,16 +181,6 @@
             row_block(0, core), row_block(SEEN_AS[place], core),
             send_rows.at[place], recv_rows.at[SEEN_AS[place]], at_x(place),
         )
-        if place == 1:
-            send(row_block(0, core), row_block(0, core), send_fwd.at[0], recv_fwd.at[0], partner)
-
-    def forward_columns(part, slot):
-        for place in range(1, LINE):
-            send(
-                col_block(0, part, slot), col_block(SEEN_AS[place], part, slot),
-                send_far.at[far_index(part, place, slot)],
-                recv_far.at[far_index(part, SEEN_AS[place], slot)], across[part](place),
-            )
 
     def wait_near(part, place):
         block = col_block(0, part, place)
@@ -180,23 +209,34 @@
         remote(block, block, send_fwd.at[chunk], recv_fwd.at[chunk], partner).wait_recv()
 
     for part in range(2):
-        forward_columns(part, 0)
+        forward_columns(part, 0, (1, 2))
 
     acc[...] = jnp.zeros_like(acc)
-    reach = lax.broadcasted_iota(jnp.int32, (16, K), 1).astype(f32) - 150.0
-    own_ids[:, 0:OWN] = lax.dot_general(
-        reach.astype(bf16), marks.astype(bf16), NT, preferred_element_type=f32
-    )
-    member[...] = jnp.where(
-        lax.broadcasted_iota(jnp.int32, (OWN, KEEP), 1).astype(f32) - 150.0 == id_column, 1.0, 0.0
-    )
-
-    for place in range(1, LINE):
+    for place in range(1, LINE - 1):
         for part in range(2):
             wait_near(part, place)
-            forward_columns(part, place)
-        if place < 3:
-            pass_rows(place)
+            forward_columns(part, place, (1, 2))
+    from_mates(info, send_info, recv_info)
+    which = lax.broadcasted_iota(jnp.int32, (KP, KEEP), 0).astype(f32) - 150.0
+    for index in range(2 * LINE):
+        side_lt[:, index * KEEP : (index + 1) * KEEP] = jnp.where(
+            which == info[index, 0:1, :], 1.0, 0.0
+        ).astype(bf16)
+    blank = jnp.zeros((1, CHUNK - KEEP), f32)
+    for chunk in range(LINE):
+        there = lax.rem(x + OFFSETS[chunk], LINE) * 2
+        first = jnp.concatenate([info[there, 0:1, :] + 1000.0, blank], axis=1)
+        second = jnp.concatenate([info[there + 1, 0:1, :] + 1000.0, blank], axis=1)
+        both = first + pltpu.roll(second, OWN, 1) - 1000.0
+        side_ids[0:1, chunk * CHUNK : (chunk + 1) * CHUNK] = both
+    pass_rows(1)
+    pass_rows(2)
+    for part in range(2):
+        wait_near(part, LINE - 1)
+        forward_columns(part, LINE - 1, (1, 2))
+    for slot in range(LINE):
+        for part in range(2):
+            forward_columns(part, slot, (LINE - 1,))
     wait_rows(0)
 
     def pair_slice(chunk, c):
@@ -265,74 +305,60 @@
         acc[:, pl.ds(side_at, TILE)] += jnp.dot(lt[...], adj[...], preferred_element_type=f32)
 
         ends = (LINE - 1) * TILES
+
+        @pl.when(t >= ends)
+        def _():
+            which = lax.broadcasted_iota(jnp.int32, (KP, TILE), 0).astype(f32) - 150.0
+            done = acc[:, pl.ds(side_at, TILE)]
+            hit = which == side_ids[0:1, pl.ds(side_at, TILE)]
+            kim_rows[0:1, pl.ds(side_at, TILE)] = jnp.sum(
+                jnp.where(hit, done, 0.0), axis=0, keepdims=True
+            )
+            kim_rows[1:2, pl.ds(side_at, TILE)] = jnp.sum(done, axis=0, keepdims=True)
+
         for after in range(1, TILES):
 
             @pl.when(t == ends + after)
             def _():
                 to_partner(LINE - after).start()
-                if after > 1:
-                    pass_sum(LINE - after + 1)
 
         return carry
 
     lax.fori_loop(0, LINE * TILES, one_tile, 0)
 
-    to_partner(0).wait_recv()
-    conn = acc[:, pl.ds(pl.multiple_of(core * 256, 128), KEEP)] + pair[0]
-    for chunk in range(1, LINE):
-        remote(
-            sent.at[chunk], got.at[chunk], send_sum.at[chunk], recv_sum.at[chunk], at_x(chunk)
-        ).wait_recv()
-        conn = conn + got[chunk].astype(f32)
-    conn = jnp.where(core == 0, conn, pltpu.roll(conn, KEEP - 64, 1))
-
-    which = lax.broadcasted_iota(jnp.int32, (KP, OWN), 0).astype(f32) - 150.0
-    valid = conn[:, 0:OWN]
-    kim = jnp.sum(jnp.where(which == own_ids[0:1, 0:OWN], valid, 0.0), axis=0, keepdims=True)
-    rowsum = jnp.sum(valid, axis=0, keepdims=True)
-    ref = ref_kim[...]
-    stacked = jnp.concatenate(
-        [kim, kim * kim, ref, ref * ref, kim * ref, rowsum, jnp.ones_like(kim), jnp.zeros_like(kim)],
-        axis=0,
-    )
-    sums = jnp.dot(
-        stacked, member[...], precision=lax.Precision.HIGHEST, preferred_element_type=f32
-    )
+    for chunk in range(LINE):
+        there = lax.rem(x + OFFSETS[chunk], LINE) * 2
+        for c in range(2):
+            for kind in range(2):
+                piece = kim_rows[kind : kind + 1, chunk * CHUNK + c * 256 : chunk * CHUNK + c * 256 + KEEP]
+                if c == 1:
+                    piece = pltpu.roll(piece, KEEP - 64, 1)
+                parts[place_xc, kind, pl.ds(there + c, 1), :] = piece
+    to_mates(parts, send_part, recv_part)
+    for chunk in range(LINE - 1, 0, -1):
+        pass_sum(chunk)
+
+    from_mates(parts, send_part, recv_part)
+    kim, rowsum = parts[0, 0], parts[0, 1]
+    for index in range(1, 2 * LINE):
+        kim = kim + parts[index, 0]
+        rowsum = rowsum + parts[index, 1]
+    for index in range(2 * LINE):
+        at = slice(index * KEEP, (index + 1) * KEEP)
+        k, r, ref = kim[index : index + 1], rowsum[index : index + 1], info[index, 1:2, :]
+        one, none = jnp.ones_like(k), jnp.zeros_like(k)
+        stats[:, at] = jnp.concatenate([k, k * k, ref, ref * ref, k * ref, r, one, none], axis=0)
+    exact = stats[...]
+    high = exact.astype(bf16).astype(f32)
+    middle = (exact - high).astype(bf16).astype(f32)
+    low = exact - high - middle
+    split = jnp.concatenate([high, middle, low, jnp.zeros_like(low)], axis=0).astype(bf16)
+    sums = lax.dot_general(split, side_lt[...], NT, preferred_element_type=f32)
+    total_sums = sums[0:8] + sums[8:16] + sums[16:24]
 
     def wait_sent(copies):
         for copy in copies:
             copy.wait_send()
-
-    place_xc = x * 2 + core
-    sums_xc[place_xc] = sums
-    copies = []
-    for place in range(LINE):
-        for flip in range(2):
-            if place == 0 and flip == 0:
-                continue
-            peer = at_x(place, core if flip == 0 else other)
-            copies.append((
-                remote(
-                    sums_xc.at[place_xc], sums_xc.at[place_xc], send_xc.at[place * 2 + flip],
-                    recv_xc.at[SEEN_AS[place] * 2 + flip], peer,
-                ),
-                place, flip,
-            ))
-    for copy, _, _ in copies:
-        copy.start()
-
-    conn_out[...] = conn.T[0:OWN, 0:K]
-
-    for copy, place, flip in copies:
-        there = lax.rem(x + OFFSETS[place], LINE) * 2 + (core if flip == 0 else other)
-        remote(
-            sums_xc.at[there], sums_xc.at[there], send_xc.at[place * 2 + flip],
-            recv_xc.at[place * 2 + flip], partner,
-        ).wait_recv()
-    total_sums = sums_xc[0]
-    for index in range(1, 2 * LINE):
-        total_sums = total_sums + sums_xc[index]
-    wait_sent([copy for copy, _, _ in copies])
 
     for axis, (mine, buffer, at) in enumerate(((y, sums_y, at_y), (z, sums_z, at_z))):
         buffer[mine] = total_sums
@@ -364,6 +390,16 @@
     between = (s_r - s_k) / (n * (float(G) - n))
     pres_out[0:1, :] = (mean_x - between) * jnp.sqrt(n / var_x)
     pres_out[1:2, :] = cross * jnp.sqrt(n / (var_x * var_y))
+
+    to_partner(0).wait_recv()
+    conn = acc[:, pl.ds(pl.multiple_of(core * 256, 128), KEEP)] + pair[0]
+    for chunk in range(1, LINE):
+        remote(
+            sent.at[chunk], got.at[chunk], send_sum.at[chunk], recv_sum.at[chunk], at_x(chunk)
+        ).wait_recv()
+        conn = conn + got[chunk].astype(f32)
+    conn = jnp.where(core == 0, conn, pltpu.roll(conn, KEEP - 64, 1))
+    conn_out[...] = conn[0:K, 0:OWN]
 
     wait_sent(started)
     for chunk in range(1, LINE):
@@ -387,22 +423,28 @@
         pltpu.VMEM((LINE, KP, KEEP), f32),
         pltpu.VMEM((LINE, KP, KEEP), bf16),
         pltpu.VMEM((LINE, KP, KEEP), bf16),
-        pltpu.VMEM((16, KEEP), f32),
-        pltpu.VMEM((OWN, KEEP), f32),
-        pltpu.VMEM((2 * LINE, 8, KEEP), f32),
-        pltpu.VMEM((LINE, 8, KEEP), f32),
-        pltpu.VMEM((LINE, 8, KEEP), f32),
+        pltpu.VMEM((2 * LINE, 2, KEEP), f32),
+        pltpu.VMEM((8, ROWS), f32),
+        pltpu.VMEM((KP, 2 * LINE * KEEP), bf16),
+        pltpu.VMEM((8, ROWS), f32),
+        pltpu.VMEM((2 * LINE, 2, 2 * LINE, KEEP), f32),
+        pltpu.VMEM((8, 2 * LINE * KEEP), f32),
+        pltpu.VMEM((LINE, 8, KP), f32),
+        pltpu.VMEM((LINE, 8, KP), f32),
     ]
-    for count in (LINE, LINE, 2 * LINE, 2 * LINE * LINE, LINE, LINE, 2 * LINE, 2 * LINE):
+    for count in (
+        LINE, LINE, 2 * LINE, 2 * LINE * LINE, LINE, LINE, 2 * LINE, 2 * LINE, 2 * LINE,
+    ):
         scratch += [dma((count,)), dma((count,))]
     return pl.pallas_call(
         functools.partial(kernel, depth, compact),
         out_shape=(
-            jax.ShapeDtypeStruct((OWN, K), f32),
+            jax.ShapeDtypeStruct((K, OWN), f32),
             jax.ShapeDtypeStruct((2, K), f32),
+            jax.ShapeDtypeStruct((1,), jnp.int32),
         ),
         in_specs=[vmem] * 4,
-        out_specs=(vmem, vmem),
+        out_specs=(vmem, vmem, pl.BlockSpec(memory_space=pltpu.SMEM)),
         scratch_shapes=scratch,
         compiler_params=pltpu.CompilerParams(
             collective_id=collective, has_side_effects=True, vmem_limit_bytes=60 * 1024 * 1024
@@ -412,17 +454,17 @@
 
 
 def local(expression, resample, labels, ref_kim):
-    samples = jnp.arange(SAMPLES, dtype=jnp.int32)
-    distinct = jnp.sum(jnp.any(resample[:, None] == samples[None, :], axis=0).astype(jnp.int32))
-    return lax.cond(
-        distinct <= 255,
-        functools.partial(whole, 256, True, 0),
-        functools.partial(whole, 512, False, 1),
-        resample.reshape(1, SAMPLES),
-        expression,
-        labels,
-        ref_kim.reshape(1, OWN),
+    operands = (
+        resample.reshape(1, SAMPLES), expression.T, labels.T, ref_kim.reshape(1, OWN),
     )
+    conn, preservation, distinct = whole(256, True, 0, *operands)
+    conn, preservation = lax.cond(
+        distinct[0] <= 255,
+        lambda *ready: ready[:2],
+        lambda *ready: whole(512, False, 1, *ready[2:])[:2],
+        conn, preservation, *operands,
+    )
+    return conn.T, preservation
 
 
 def solution(mesh):

time: 78.1 us -> 62.8 us (0.80); the launches traced: 77.1 us -> 62.7 us
  Pallas kernels: 68 us -> 59.3 us
  local copies, waits for them, and re-layouts: 6.25 us -> 2.04 us
  other arithmetic: 1.48 us -> 0 us
    pallas_call x1, Pallas kernels: 68 us -> 59.3 us  [whole(): pl.pallas_call(functools.partial(kernel, depth, compact), out_shape=(jax....]
    another operation x2 -> x0, local copies, waits for them, and re-layouts: 3.09 us -> none
    unnamed x7 -> x10, local copies, waits for them, and re-layouts: 0.79 us -> 2.03 us
    cond x3 -> x0, local copies, waits for them, and re-layouts: 1.24 us -> none  [the longest x1 1.24 us: local(): lax.cond(distinct <= 255, functools.partial(whole, 256, True, 0), functoo...]
    reduce_or x1 -> x0, other arithmetic: 0.84 us -> none  [local(): jnp.any(resample[:, None] == samples[None, :], axis=0).astype(jnp.int32)]
where the time goes in v2:
time: 62.8 us; the launch traced here: 62.7 us
  Pallas kernels  59.3 us (94%)
  local copies, waits for them, and re-layouts  2.04 us (3%)
  between operations  1.37 us (2%)
    pallas_call x1, Pallas kernels, whole(): pl.pallas_call(functools.partial(kernel, depth, compact), out_shape=(jax....  59.3 us
    unnamed x10, local copies, waits for them, and re-layouts  2.03 us

profile of v2, /device:TPU:1, one launch (start us, length us, event | category | flops | bytes accessed | tf_op | source)
XLA Modules:
  0.0 62.7 jit_solution(13330620697899439151)
XLA Ops:
  0.6 0.0 copy-start.2
  0.6 0.0 copy-start.3
  0.6 0.7 %copy-done.2 = s32[384]{0:T(512)S(1)} copy-done((s32[384]{0:T(512)S(1)}, s32[384]{0:T(512)}, u32[]{:S(2)}) %copy-start.2) | copy-done | bytes 1560
  1.3 0.0 copy-start
  1.3 0.0 copy-done.3
  1.3 0.0 copy-start.1
  1.3 59.3 %network_256.1 = (f32[300,320]{1,0:T(8,128)S(1)}, f32[2,300]{1,0:T(2,128)S(1)}, s32[1]{0:T(128)}) custom-call(s32[1,384]{1,0:T(1,128)S(1)} %reshape.14.resample, f32[320,384]{1,0:T(8,128)} %bitcast.4, s32[300,320]{1,0:T(8,128)} %bitcast.6, f32[1,320]{1,0:T(1,128)S(1)} %reshape.15.ref_kim), custom_call_target="tpu_custom_call" | custom-call | tf_op jit(solution)/shard_map/network_256/pallas_call | solution.py:439
  61.3 0.0 copy-done
  61.3 0.0 copy-done.1
  61.3 0.8 %copy.12 = f32[320,300]{0,1:T(8,128)} copy(f32[320,300]{0,1:T(8,128)S(1)} %bitcast.8) | data formatting | bytes 768000
  62.1 0.6 copy.13
  (3 shorter events, 0.0 us)
Async XLA Ops:
  0.6 0.7 %copy-start.2 = (s32[384]{0:T(512)S(1)}, s32[384]{0:T(512)}, u32[]{:S(2)}) copy-start(s32[384]{0:T(512)} %param.7) | copy-start | bytes 4612
  0.6 0.7 %copy-start.3 = (f32[320]{0:T(512)S(1)}, f32[320]{0:T(512)}, u32[]{:S(2)}) copy-start(f32[320]{0:T(512)} %param.9) | copy-start | bytes 3844
  1.3 60.0 %copy-start = (f32[384,320]{0,1:T(8,128)S(1)}, f32[384,320]{0,1:T(8,128)}, u32[]{:S(2)}) copy-start(f32[384,320]{0,1:T(8,128)} %param.6) | copy-start | bytes 1474564
  1.3 60.0 %copy-start.1 = (s32[320,300]{0,1:T(8,128)S(1)}, s32[320,300]{0,1:T(8,128)}, u32[]{:S(2)}) copy-start(s32[320,300]{0,1:T(8,128)} %param.8) | copy-start | bytes 1152004

commit v3 on v2

--- a/solution.py
+++ b/solution.py
@@ -16,9 +16,10 @@
 HALF = OWN // 2
 LINE = 4
 CHUNK = 2 * OWN
-STEP = 2 * LINE * HALF
+EARLY = 2 * (LINE - 1) * HALF
+LATE = 2 * LINE * HALF
 ROWS = LINE * CHUNK
-COLS = LINE * STEP
+COLS = LINE * EARLY + LATE
 TILE = 512
 TILES = ROWS // TILE
 KEEP = 384
@@ -30,8 +31,8 @@
 
 def kernel(
     depth, compact, resample, expression, labels, ref_kim, conn_out, pres_out, count_out,
-    rows, cols, lt, adj, acc, pair, sent, got, info, side_ids, side_lt, kim_rows, parts, stats,
-    sums_y, sums_z,
+    values_in, labels_in, rows, cols, lt, lt_late, even, odd, acc, pair, sent, got, info, side_ids, side_lt,
+    kim_rows, parts, stats, sums_y, sums_z, loaded,
     send_rows, recv_rows, send_fwd, recv_fwd, send_near, recv_near, send_far, recv_far,
     send_pair, recv_pair, send_sum, recv_sum, send_info, recv_info, send_part, recv_part,
     send_yz, recv_yz,
@@ -56,6 +57,10 @@
 
     partner = {"c": other}
 
+    load_values = pltpu.make_async_copy(expression, values_in, loaded.at[0])
+    load_labels = pltpu.make_async_copy(labels, labels_in, loaded.at[1])
+    load_values.start()
+    load_labels.start()
     barrier = pltpu.get_barrier_semaphore()
     peers = [partner]
     for place in range(1, LINE):
@@ -95,7 +100,8 @@
     pick = jnp.where(
         lax.broadcasted_iota(jnp.int32, (depth, SAMPLES), 0) == place_of, 1.0, 0.0
     ).astype(bf16)
-    values = expression[...]
+    load_values.wait()
+    values = values_in[...]
     mean = jnp.sum(values * times, axis=1, keepdims=True) * (1.0 / SAMPLES)
     centered = values - mean
     total = jnp.sum(centered * centered * times, axis=1, keepdims=True)
@@ -103,7 +109,8 @@
     weighted = (scaled.astype(f32) * times).astype(bf16)
     side = lax.dot_general(weighted, pick, NT, preferred_element_type=f32)
     front = lax.dot_general(scaled, pick, NT, preferred_element_type=f32)
-    marks = labels[...].astype(f32)
+    load_labels.wait()
+    marks = labels_in[...].astype(f32)
     module = lax.broadcasted_iota(jnp.int32, (K, depth), 0).astype(f32) - 150.0
     module = jnp.where(lax.broadcasted_iota(jnp.int32, (K, depth), 1) == depth - 1, module, 0.0)
     front = front + lax.dot_general(
@@ -113,7 +120,7 @@
     front = front.astype(bf16)
     rows[pl.ds(pl.multiple_of(core * OWN, OWN), OWN), :] = side.astype(bf16)
     cols[0:HALF, :] = front[0:HALF]
-    cols[STEP // 2 : STEP // 2 + HALF, :] = front[HALF:OWN]
+    cols[EARLY // 2 : EARLY // 2 + HALF, :] = front[HALF:OWN]
     place_xc = x * 2 + core
     module = lax.broadcasted_iota(jnp.int32, (K, OWN), 0).astype(f32) - 150.0
     info[place_xc, 0:1, :] = jnp.full((1, KEEP), -1000.0, f32)
@@ -127,7 +134,13 @@
         return rows.at[pl.ds(pl.multiple_of(chunk * CHUNK + c * OWN, OWN), OWN), :]
 
     def col_block(step, part, slot):
-        return cols.at[pl.ds(step * STEP + part * (STEP // 2) + slot * HALF, HALF), :]
+        if step == LINE - 1:
+            at = LINE * EARLY + part * (LATE // 2) + slot * HALF
+        elif slot == LINE - 1:
+            at = (LINE - 1) * EARLY + step * OWN + part * HALF
+        else:
+            at = step * EARLY + part * (EARLY // 2) + slot * HALF
+        return cols.at[pl.ds(at, HALF), :]
 
     def near_index(part, place):
         return part * LINE + place
@@ -160,27 +173,35 @@
                 recv_sem.at[place * 2 + flip], group(place, flip),
             ).wait_recv()
 
+    def far_copy(part, slot, place):
+        return remote(
+            col_block(0, part, slot), col_block(SEEN_AS[place], part, slot),
+            send_far.at[far_index(part, place, slot)],
+            recv_far.at[far_index(part, SEEN_AS[place], slot)], across[part](place),
+        )
+
     def forward_columns(part, slot, places):
         for place in places:
-            send(
-                col_block(0, part, slot), col_block(SEEN_AS[place], part, slot),
-                send_far.at[far_index(part, place, slot)],
-                recv_far.at[far_index(part, SEEN_AS[place], slot)], across[part](place),
-            )
-
-    to_mates(info, send_info, recv_info)
-    send(row_block(0, core), row_block(0, core), send_fwd.at[0], recv_fwd.at[0], partner)
-    for place in range(1, LINE):
+            far_copy(part, slot, place).start()
+
+    def send_near_columns(place):
         for part in range(2):
             send(
                 col_block(0, part, 0), col_block(0, part, SEEN_AS[place]),
                 send_near.at[near_index(part, place)],
                 recv_near.at[near_index(part, SEEN_AS[place])], along[part](place),
             )
+
+    for place in range(1, LINE):
+        if place < LINE - 1:
+            send_near_columns(place)
         send(
             row_block(0, core), row_block(SEEN_AS[place], core),
             send_rows.at[place], recv_rows.at[SEEN_AS[place]], at_x(place),
         )
+        if place == 1:
+            send(row_block(0, core), row_block(0, core), send_fwd.at[0], recv_fwd.at[0], partner)
+    to_mates(info, send_info, recv_info)
 
     def wait_near(part, place):
         block = col_block(0, part, place)
@@ -189,9 +210,9 @@
             recv_near.at[near_index(part, place)], along[part](place),
         ).wait_recv()
 
-    def wait_far(step):
+    def wait_far(step, slots):
         for part in range(2):
-            for slot in range(LINE):
+            for slot in slots:
                 block = col_block(step, part, slot)
                 remote(
                     block, block, send_far.at[far_index(part, step, slot)],
@@ -216,28 +237,26 @@
         for part in range(2):
             wait_near(part, place)
             forward_columns(part, place, (1, 2))
-    from_mates(info, send_info, recv_info)
-    which = lax.broadcasted_iota(jnp.int32, (KP, KEEP), 0).astype(f32) - 150.0
-    for index in range(2 * LINE):
-        side_lt[:, index * KEEP : (index + 1) * KEEP] = jnp.where(
-            which == info[index, 0:1, :], 1.0, 0.0
-        ).astype(bf16)
-    blank = jnp.zeros((1, CHUNK - KEEP), f32)
-    for chunk in range(LINE):
-        there = lax.rem(x + OFFSETS[chunk], LINE) * 2
-        first = jnp.concatenate([info[there, 0:1, :] + 1000.0, blank], axis=1)
-        second = jnp.concatenate([info[there + 1, 0:1, :] + 1000.0, blank], axis=1)
-        both = first + pltpu.roll(second, OWN, 1) - 1000.0
-        side_ids[0:1, chunk * CHUNK : (chunk + 1) * CHUNK] = both
-    pass_rows(1)
-    pass_rows(2)
-    for part in range(2):
-        wait_near(part, LINE - 1)
-        forward_columns(part, LINE - 1, (1, 2))
-    for slot in range(LINE):
+    send_near_columns(LINE - 1)
+    for slot in range(LINE - 1):
         for part in range(2):
             forward_columns(part, slot, (LINE - 1,))
     wait_rows(0)
+
+    def take_info():
+        from_mates(info, send_info, recv_info)
+        which = lax.broadcasted_iota(jnp.int32, (KP, KEEP), 0).astype(f32) - 150.0
+        for index in range(2 * LINE):
+            side_lt[:, index * KEEP : (index + 1) * KEEP] = jnp.where(
+                which == info[index, 0:1, :], 1.0, 0.0
+            ).astype(bf16)
+        blank = jnp.zeros((1, CHUNK - KEEP), f32)
+        for chunk in range(LINE):
+            there = lax.rem(x + OFFSETS[chunk], LINE) * 2
+            first = jnp.concatenate([info[there, 0:1, :] + 1000.0, blank], axis=1)
+            second = jnp.concatenate([info[there + 1, 0:1, :] + 1000.0, blank], axis=1)
+            both = first + pltpu.roll(second, OWN, 1) - 1000.0
+            side_ids[0:1, chunk * CHUNK : (chunk + 1) * CHUNK] = both
 
     def pair_slice(chunk, c):
         return acc.at[:, pl.ds(pl.multiple_of(chunk * CHUNK + c * 256, 128), KEEP)]
@@ -260,71 +279,113 @@
         sent[chunk] = (mine + pair[chunk]).astype(bf16)
         to_owner(chunk).start()
 
-    def one_tile(t, carry):
-        step, turn = t // TILES, lax.rem(t, TILES)
-        tile = jnp.where(step == LINE - 1, TILES - 1 - turn, turn)
-        base = pl.multiple_of(step * STEP, STEP)
-        side_at = pl.multiple_of(tile * TILE, TILE)
-
-        @pl.when(t == 1)
+    def make_labels(base, width):
+        last = lax.broadcasted_iota(jnp.int32, (16, depth), 1) == depth - 1
+        ids = lax.dot_general(
+            jnp.where(last, 1.0, 0.0).astype(bf16), cols[pl.ds(base, width), :], NT,
+            preferred_element_type=f32,
+        )
+        which = lax.broadcasted_iota(jnp.int32, (KP, width), 0).astype(f32) - 150.0
+        return jnp.where(which == ids[0:1, :], 1.0, 0.0).astype(bf16)
+
+    def score(into, base, width, side_at):
+        side_block = rows[pl.ds(side_at, TILE), :]
+        for start in range(0, width, 256):
+            size = min(256, width - start)
+            scores = lax.dot_general(
+                cols[pl.ds(base + start, size), :], side_block, NT, preferred_element_type=f32
+            )
+            squares = scores * scores
+            into[start : start + size, :] = (squares * squares * squares).astype(bf16)
+
+    def count(held, width, side_at, module_rows):
+        acc[:, pl.ds(side_at, TILE)] += jnp.dot(
+            module_rows, held[0:width, :], preferred_element_type=f32
+        )
+
+    soon = (LINE - 1) * 3
+    later = soon + (LINE - 1) * 2
+
+    def task(t):
+        group = jnp.where(
+            t < soon, t // 3, jnp.where(t < later, (t - soon) // 2, LINE - 1)
+        )
+        tile = jnp.where(
+            t < soon, lax.rem(t, 3), jnp.where(t < later, 3 + lax.rem(t + 1, 2), t - later)
+        )
+        return group, pl.multiple_of(group * EARLY, HALF), pl.multiple_of(tile * TILE, TILE)
+
+    def score_task(into, t):
+        group, base, side_at = task(t)
+        score(into, base, EARLY, side_at)
+
+    def count_task(held, t):
+        group, base, side_at = task(t)
+        count(held, EARLY, side_at, lt[group])
+
+    lt[0] = make_labels(0, EARLY)
+    score_task(even, 0)
+    pass_rows(1)
+    pass_rows(2)
+    take_info()
+
+    def two_tiles(u, carry):
+        @pl.when(u == 0)
         def _():
             wait_rows(1)
-
-        @pl.when(t == 2)
-        def _():
-            pass_rows(3)
             wait_rows(2)
 
-        @pl.when(t == 3)
+        for far in range(1, LINE - 1):
+
+            @pl.when(u == far)
+            def _():
+                wait_far(far, range(LINE - 1))
+                lt[far] = make_labels(far * EARLY, EARLY)
+                if far == LINE - 2:
+                    for part in range(2):
+                        wait_near(part, LINE - 1)
+                        forward_columns(part, LINE - 1, (1, 2, 3))
+                    pass_rows(3)
+
+        @pl.when(u == (soon - 1) // 2)
         def _():
             wait_rows(3)
 
-        for far in range(1, LINE):
-
-            @pl.when(t == far * TILES)
-            def _():
-                wait_far(far)
-
-        @pl.when(turn == 0)
+        @pl.when(u == (later - 1) // 2)
         def _():
-            last = lax.broadcasted_iota(jnp.int32, (16, depth), 1) == depth - 1
-            ids = lax.dot_general(
-                jnp.where(last, 1.0, 0.0).astype(bf16), cols[pl.ds(base, STEP), :], NT,
-                preferred_element_type=f32,
-            )
-            which = lax.broadcasted_iota(jnp.int32, (KP, STEP), 0).astype(f32) - 150.0
-            lt[...] = jnp.where(which == ids[0:1, :], 1.0, 0.0).astype(bf16)
-
-        side_block = rows[pl.ds(side_at, TILE), :]
-        for part in range(STEP // 256):
-            scores = lax.dot_general(
-                cols[pl.ds(base + part * 256, 256), :], side_block, NT, preferred_element_type=f32
-            )
-            squares = scores * scores
-            adj[part * 256 : (part + 1) * 256, :] = (squares * squares * squares).astype(bf16)
-        acc[:, pl.ds(side_at, TILE)] += jnp.dot(lt[...], adj[...], preferred_element_type=f32)
-
-        ends = (LINE - 1) * TILES
-
-        @pl.when(t >= ends)
-        def _():
-            which = lax.broadcasted_iota(jnp.int32, (KP, TILE), 0).astype(f32) - 150.0
-            done = acc[:, pl.ds(side_at, TILE)]
-            hit = which == side_ids[0:1, pl.ds(side_at, TILE)]
-            kim_rows[0:1, pl.ds(side_at, TILE)] = jnp.sum(
-                jnp.where(hit, done, 0.0), axis=0, keepdims=True
-            )
-            kim_rows[1:2, pl.ds(side_at, TILE)] = jnp.sum(done, axis=0, keepdims=True)
-
-        for after in range(1, TILES):
-
-            @pl.when(t == ends + after)
-            def _():
-                to_partner(LINE - after).start()
-
+            wait_far(1, (LINE - 1,))
+            wait_far(2, (LINE - 1,))
+            lt[LINE - 1] = make_labels((LINE - 1) * EARLY, EARLY)
+
+        count_task(even, 2 * u)
+        score_task(odd, 2 * u + 1)
+        count_task(odd, 2 * u + 1)
+        score_task(even, 2 * u + 2)
         return carry
 
-    lax.fori_loop(0, LINE * TILES, one_tile, 0)
+    pairs = (later + TILES - 2) // 2
+    lax.fori_loop(0, pairs, two_tiles, 0)
+    count_task(even, 2 * pairs)
+    score_task(odd, 2 * pairs + 1)
+    wait_far(LINE - 1, range(LINE))
+    lt_late[...] = make_labels(LINE * EARLY, LATE)
+    count_task(odd, 2 * pairs + 1)
+    score(even, LINE * EARLY, LATE, (TILES - 1) * TILE)
+    for turn in range(TILES):
+        side_at = (TILES - 1 - turn) * TILE
+        held, into = (even, odd) if turn % 2 == 0 else (odd, even)
+        count(held, LATE, side_at, lt_late[...])
+        if turn < TILES - 1:
+            score(into, LINE * EARLY, LATE, side_at - TILE)
+        which = lax.broadcasted_iota(jnp.int32, (KP, TILE), 0).astype(f32) - 150.0
+        done = acc[:, side_at : side_at + TILE]
+        hit = which == side_ids[0:1, side_at : side_at + TILE]
+        kim_rows[0:1, side_at : side_at + TILE] = jnp.sum(
+            jnp.where(hit, done, 0.0), axis=0, keepdims=True
+        )
+        kim_rows[1:2, side_at : side_at + TILE] = jnp.sum(done, axis=0, keepdims=True)
+        if turn > 0:
+            to_partner(LINE - turn).start()
 
     for chunk in range(LINE):
         there = lax.rem(x + OFFSETS[chunk], LINE) * 2
@@ -402,6 +463,10 @@
     conn_out[...] = conn[0:K, 0:OWN]
 
     wait_sent(started)
+    for place in range(1, LINE):
+        for part in range(2):
+            for slot in range(LINE):
+                far_copy(part, slot, place).wait_send()
     for chunk in range(1, LINE):
         block = row_block(chunk, core)
         remote(block, block, send_fwd.at[chunk], recv_fwd.at[chunk], partner).wait_send()
@@ -413,12 +478,16 @@
 def whole(depth, compact, collective, resample, expression, labels, ref_kim):
     f32, bf16 = jnp.float32, jnp.bfloat16
     dma = pltpu.SemaphoreType.DMA
-    vmem = pl.BlockSpec(memory_space=pltpu.VMEM)
+    vmem, hbm = pl.BlockSpec(memory_space=pltpu.VMEM), pl.BlockSpec(memory_space=pl.ANY)
     scratch = [
+        pltpu.VMEM((OWN, SAMPLES), f32),
+        pltpu.VMEM((K, OWN), jnp.int32),
         pltpu.VMEM((ROWS, depth), bf16),
         pltpu.VMEM((COLS, depth), bf16),
-        pltpu.VMEM((KP, STEP), bf16),
-        pltpu.VMEM((STEP, TILE), bf16),
+        pltpu.VMEM((LINE, KP, EARLY), bf16),
+        pltpu.VMEM((KP, LATE), bf16),
+        pltpu.VMEM((LATE, TILE), bf16),
+        pltpu.VMEM((LATE, TILE), bf16),
         pltpu.VMEM((KP, ROWS), f32),
         pltpu.VMEM((LINE, KP, KEEP), f32),
         pltpu.VMEM((LINE, KP, KEEP), bf16),
@@ -431,6 +500,7 @@
         pltpu.VMEM((8, 2 * LINE * KEEP), f32),
         pltpu.VMEM((LINE, 8, KP), f32),
         pltpu.VMEM((LINE, 8, KP), f32),
+        dma((2,)),
     ]
     for count in (
         LINE, LINE, 2 * LINE, 2 * LINE * LINE, LINE, LINE, 2 * LINE, 2 * LINE, 2 * LINE,
@@ -443,7 +513,7 @@
             jax.ShapeDtypeStruct((2, K), f32),
             jax.ShapeDtypeStruct((1,), jnp.int32),
         ),
-        in_specs=[vmem] * 4,
+        in_specs=[vmem, hbm, hbm, vmem],
         out_specs=(vmem, vmem, pl.BlockSpec(memory_space=pltpu.SMEM)),
         scratch_shapes=scratch,
         compiler_params=pltpu.CompilerParams(

time: 62.8 us -> 60.8 us (0.968)
  Pallas kernels: 59.3 us -> 56.6 us
    pallas_call x1, Pallas kernels: 59.3 us -> 56.6 us  [whole(): pl.pallas_call(functools.partial(kernel, depth, compact), out_shape=(jax....]
where the time goes in v3:
time: 60.8 us; the launch traced here: 60.2 us
  Pallas kernels  56.6 us (93%)
  local copies, waits for them, and re-layouts  2.04 us (3%)
  between operations  1.37 us (2%)
    pallas_call x1, Pallas kernels, whole(): pl.pallas_call(functools.partial(kernel, depth, compact), out_shape=(jax....  56.6 us
    unnamed x10, local copies, waits for them, and re-layouts  2.03 us

profile of v3, /device:TPU:1, one launch (start us, length us, event | category | flops | bytes accessed | tf_op | source)
XLA Modules:
  0.0 60.2 jit_solution(17007181931172338707)
XLA Ops:
  0.6 0.0 copy-start.2
  0.6 0.0 copy-start.3
  0.6 0.7 %copy-done.2 = s32[384]{0:T(512)S(1)} copy-done((s32[384]{0:T(512)S(1)}, s32[384]{0:T(512)}, u32[]{:S(2)}) %copy-start.2) | copy-done | bytes 1560
  1.3 0.0 copy-start
  1.3 0.0 copy-done.3
  1.3 0.0 copy-start.1
  1.3 56.6 %network_256.1 = (f32[300,320]{1,0:T(8,128)S(1)}, f32[2,300]{1,0:T(2,128)S(1)}, s32[1]{0:T(128)}) custom-call(s32[1,384]{1,0:T(1,128)S(1)} %reshape.14.resample, f32[320,384]{1,0:T(8,128)} %bitcast.4, s32[300,320]{1,0:T(8,128)} %bitcast.6, f32[1,320]{1,0:T(1,128)S(1)} %reshape.15.ref_kim), custom_call_target="tpu_custom_call" | custom-call | tf_op jit(solution)/shard_map/network_256/pallas_call | solution.py:509
  58.6 0.0 copy-done
  58.6 0.0 copy-done.1
  58.6 0.2 conditional.1
  58.9 0.8 %copy.12 = f32[320,300]{0,1:T(8,128)} copy(f32[320,300]{0,1:T(8,128)S(1)} %bitcast.8) | data formatting | bytes 768000
  59.6 0.6 copy.13
  (2 shorter events, 0.0 us)
Async XLA Ops:
  0.6 0.7 %copy-start.2 = (s32[384]{0:T(512)S(1)}, s32[384]{0:T(512)}, u32[]{:S(2)}) copy-start(s32[384]{0:T(512)} %param.7) | copy-start | bytes 4612
  0.6 0.7 %copy-start.3 = (f32[320]{0:T(512)S(1)}, f32[320]{0:T(512)}, u32[]{:S(2)}) copy-start(f32[320]{0:T(512)} %param.9) | copy-start | bytes 3844
  1.3 57.3 %copy-start = (f32[384,320]{0,1:T(8,128)S(1)}, f32[384,320]{0,1:T(8,128)}, u32[]{:S(2)}) copy-start(f32[384,320]{0,1:T(8,128)} %param.6) | copy-start | bytes 1474564
  1.3 57.3 %copy-start.1 = (s32[320,300]{0,1:T(8,128)S(1)}, s32[320,300]{0,1:T(8,128)}, u32[]{:S(2)}) copy-start(s32[320,300]{0,1:T(8,128)} %param.8) | copy-start | bytes 1152004

commit v4 on v3

--- a/solution.py
+++ b/solution.py
@@ -192,17 +192,19 @@
                 recv_near.at[near_index(part, SEEN_AS[place])], along[part](place),
             )
 
-    for place in range(1, LINE):
-        if place < LINE - 1:
-            send_near_columns(place)
+    def send_rows_to(place):
         send(
             row_block(0, core), row_block(SEEN_AS[place], core),
             send_rows.at[place], recv_rows.at[SEEN_AS[place]], at_x(place),
         )
-        if place == 1:
-            send(row_block(0, core), row_block(0, core), send_fwd.at[0], recv_fwd.at[0], partner)
+
+    def own_rows():
+        send(row_block(0, core), row_block(0, core), send_fwd.at[0], recv_fwd.at[0], partner)
+
+    send_near_columns(1)
+    send_near_columns(2)
+    own_rows()
     to_mates(info, send_info, recv_info)
-
     def wait_near(part, place):
         block = col_block(0, part, place)
         remote(
@@ -231,6 +233,9 @@
 
     for part in range(2):
         forward_columns(part, 0, (1, 2))
+    send_rows_to(1)
+    send_rows_to(2)
+    send_rows_to(3)
 
     acc[...] = jnp.zeros_like(acc)
     for place in range(1, LINE - 1):

time: 60.8 us -> 58.4 us (0.961)
  Pallas kernels: 56.6 us -> 54.6 us
    pallas_call x1, Pallas kernels: 56.6 us -> 54.6 us  [whole(): pl.pallas_call(functools.partial(kernel, depth, compact), out_shape=(jax....]
where the time goes in v4:
time: 58.4 us; the launch traced here: 58.2 us
  Pallas kernels  54.6 us (93%)
  local copies, waits for them, and re-layouts  2.04 us (3%)
  between operations  1.37 us (2%)
    pallas_call x1, Pallas kernels, whole(): pl.pallas_call(functools.partial(kernel, depth, compact), out_shape=(jax....  54.6 us
    unnamed x10, local copies, waits for them, and re-layouts  2.03 us

profile of v4, /device:TPU:1, one launch (start us, length us, event | category | flops | bytes accessed | tf_op | source)
XLA Modules:
  0.0 58.2 jit_solution(10160791830187950568)
XLA Ops:
  0.6 0.0 copy-start.2
  0.6 0.0 copy-start.3
  0.6 0.7 %copy-done.2 = s32[384]{0:T(512)S(1)} copy-done((s32[384]{0:T(512)S(1)}, s32[384]{0:T(512)}, u32[]{:S(2)}) %copy-start.2) | copy-done | bytes 1560
  1.3 0.0 copy-start
  1.3 0.0 copy-done.3
  1.3 0.0 copy-start.1
  1.3 54.6 %network_256.1 = (f32[300,320]{1,0:T(8,128)S(1)}, f32[2,300]{1,0:T(2,128)S(1)}, s32[1]{0:T(128)}) custom-call(s32[1,384]{1,0:T(1,128)S(1)} %reshape.14.resample, f32[320,384]{1,0:T(8,128)} %bitcast.4, s32[300,320]{1,0:T(8,128)} %bitcast.6, f32[1,320]{1,0:T(1,128)S(1)} %reshape.15.ref_kim), custom_call_target="tpu_custom_call" | custom-call | tf_op jit(solution)/shard_map/network_256/pallas_call | solution.py:514
  56.6 0.0 copy-done
  56.6 0.0 copy-done.1
  56.6 0.2 conditional.1
  56.8 0.8 %copy.12 = f32[320,300]{0,1:T(8,128)} copy(f32[320,300]{0,1:T(8,128)S(1)} %bitcast.8) | data formatting | bytes 768000
  57.6 0.6 copy.13
  (2 shorter events, 0.0 us)
Async XLA Ops:
  0.6 0.7 %copy-start.2 = (s32[384]{0:T(512)S(1)}, s32[384]{0:T(512)}, u32[]{:S(2)}) copy-start(s32[384]{0:T(512)} %param.7) | copy-start | bytes 4612
  0.6 0.7 %copy-start.3 = (f32[320]{0:T(512)S(1)}, f32[320]{0:T(512)}, u32[]{:S(2)}) copy-start(f32[320]{0:T(512)} %param.9) | copy-start | bytes 3844
  1.3 55.3 %copy-start = (f32[384,320]{0,1:T(8,128)S(1)}, f32[384,320]{0,1:T(8,128)}, u32[]{:S(2)}) copy-start(f32[384,320]{0,1:T(8,128)} %param.6) | copy-start | bytes 1474564
  1.3 55.3 %copy-start.1 = (s32[320,300]{0,1:T(8,128)S(1)}, s32[320,300]{0,1:T(8,128)}, u32[]{:S(2)}) copy-start(s32[320,300]{0,1:T(8,128)} %param.8) | copy-start | bytes 1152004

commit v5 on v4

--- a/solution.py
+++ b/solution.py
@@ -31,7 +31,7 @@
 
 def kernel(
     depth, compact, resample, expression, labels, ref_kim, conn_out, pres_out, count_out,
-    values_in, labels_in, rows, cols, lt, lt_late, even, odd, acc, pair, sent, got, info, side_ids, side_lt,
+    values_in, labels_in, rows, cols, lt, lt_late, even, odd, acc, pair, sent, got, sent_shared, got_shared, info, side_ids, side_lt,
     kim_rows, parts, stats, sums_y, sums_z, loaded,
     send_rows, recv_rows, send_fwd, recv_fwd, send_near, recv_near, send_far, recv_far,
     send_pair, recv_pair, send_sum, recv_sum, send_info, recv_info, send_part, recv_part,
@@ -272,17 +272,33 @@
             partner,
         )
 
+    ours = (lax.broadcasted_iota(jnp.int32, (KP // 2, 128), 1) < 64) == (core == 0)
+
+    def summed(chunk):
+        whole_at = pl.multiple_of(chunk * CHUNK + core * 384, 128)
+        main = acc[:, pl.ds(whole_at, 256)]
+        main = main + pair[chunk, :, pl.ds(pl.multiple_of(core * 128, 128), 256)]
+        shared = acc[:, chunk * CHUNK + 256 : chunk * CHUNK + 384]
+        shared = shared + pair[chunk, :, pl.ds(pl.multiple_of((1 - core) * 256, 128), 128)]
+        return main, shared
+
     def to_owner(chunk):
-        return remote(
-            sent.at[chunk], got.at[SEEN_AS[chunk]], send_sum.at[chunk],
-            recv_sum.at[SEEN_AS[chunk]], at_x(chunk),
-        )
+        return [
+            remote(
+                src.at[chunk], dst.at[SEEN_AS[chunk]], send_sum.at[first + chunk],
+                recv_sum.at[first + SEEN_AS[chunk]], at_x(chunk),
+            )
+            for src, dst, first in ((sent, got, 0), (sent_shared, got_shared, LINE))
+        ]
 
     def pass_sum(chunk):
         to_partner(chunk).wait_recv()
-        mine = acc[:, pl.ds(pl.multiple_of(chunk * CHUNK + core * 256, 128), KEEP)]
-        sent[chunk] = (mine + pair[chunk]).astype(bf16)
-        to_owner(chunk).start()
+        main, shared = summed(chunk)
+        sent[chunk] = main.astype(bf16)
+        upper = pltpu.roll(shared[KP // 2 : KP], 64, 1)
+        sent_shared[chunk] = jnp.where(ours, shared[0 : KP // 2], upper).astype(bf16)
+        for copy in to_owner(chunk):
+            copy.start()
 
     def make_labels(base, width):
         last = lax.broadcasted_iota(jnp.int32, (16, depth), 1) == depth - 1
@@ -458,13 +474,21 @@
     pres_out[1:2, :] = cross * jnp.sqrt(n / (var_x * var_y))
 
     to_partner(0).wait_recv()
-    conn = acc[:, pl.ds(pl.multiple_of(core * 256, 128), KEEP)] + pair[0]
+    main, shared = summed(0)
     for chunk in range(1, LINE):
-        remote(
-            sent.at[chunk], got.at[chunk], send_sum.at[chunk], recv_sum.at[chunk], at_x(chunk)
-        ).wait_recv()
-        conn = conn + got[chunk].astype(f32)
-    conn = jnp.where(core == 0, conn, pltpu.roll(conn, KEEP - 64, 1))
+        for src, dst, first in ((sent, got, 0), (sent_shared, got_shared, LINE)):
+            remote(
+                src.at[chunk], dst.at[chunk], send_sum.at[first + chunk],
+                recv_sum.at[first + chunk], at_x(chunk),
+            ).wait_recv()
+        main = main + got[chunk].astype(f32)
+        lower = got_shared[chunk].astype(f32)
+        shared = shared + jnp.concatenate([lower, pltpu.roll(lower, 64, 1)], axis=0)
+    conn = jnp.where(
+        core == 0,
+        jnp.concatenate([main, shared], axis=1),
+        pltpu.roll(jnp.concatenate([shared, main], axis=1), KEEP - 64, 1),
+    )
     conn_out[...] = conn[0:K, 0:OWN]
 
     wait_sent(started)
@@ -475,7 +499,8 @@
     for chunk in range(1, LINE):
         block = row_block(chunk, core)
         remote(block, block, send_fwd.at[chunk], recv_fwd.at[chunk], partner).wait_send()
-        to_owner(chunk).wait_send()
+        for copy in to_owner(chunk):
+            copy.wait_send()
     for chunk in range(LINE):
         to_partner(chunk).wait_send()
 
@@ -495,8 +520,10 @@
         pltpu.VMEM((LATE, TILE), bf16),
         pltpu.VMEM((KP, ROWS), f32),
         pltpu.VMEM((LINE, KP, KEEP), f32),
-        pltpu.VMEM((LINE, KP, KEEP), bf16),
-        pltpu.VMEM((LINE, KP, KEEP), bf16),
+        pltpu.VMEM((LINE, KP, 256), bf16),
+        pltpu.VMEM((LINE, KP, 256), bf16),
+        pltpu.VMEM((LINE, KP // 2, 128), bf16),
+        pltpu.VMEM((LINE, KP // 2, 128), bf16),
         pltpu.VMEM((2 * LINE, 2, KEEP), f32),
         pltpu.VMEM((8, ROWS), f32),
         pltpu.VMEM((KP, 2 * LINE * KEEP), bf16),
@@ -508,7 +535,7 @@
         dma((2,)),
     ]
     for count in (
-        LINE, LINE, 2 * LINE, 2 * LINE * LINE, LINE, LINE, 2 * LINE, 2 * LINE, 2 * LINE,
+        LINE, LINE, 2 * LINE, 2 * LINE * LINE, LINE, 2 * LINE, 2 * LINE, 2 * LINE, 2 * LINE,
     ):
         scratch += [dma((count,)), dma((count,))]
     return pl.pallas_call(

time: 58.4 us -> 57.3 us (0.981)
  Pallas kernels: 54.6 us -> 53.5 us
    pallas_call x1, Pallas kernels: 54.6 us -> 53.5 us  [whole(): pl.pallas_call(functools.partial(kernel, depth, compact), out_shape=(jax....]
where the time goes in v5:
time: 57.3 us; the launch traced here: 57.1 us
  Pallas kernels  53.5 us (93%)
  local copies, waits for them, and re-layouts  2.04 us (4%)
  between operations  1.37 us (2%)
    pallas_call x1, Pallas kernels, whole(): pl.pallas_call(functools.partial(kernel, depth, compact), out_shape=(jax....  53.5 us
    unnamed x10, local copies, waits for them, and re-layouts  2.03 us

profile of v5, /device:TPU:1, one launch (start us, length us, event | category | flops | bytes accessed | tf_op | source)
XLA Modules:
  0.0 57.1 jit_solution(1686919537795048360)
XLA Ops:
  0.6 0.0 copy-start.2
  0.6 0.0 copy-start.3
  0.6 0.7 %copy-done.2 = s32[384]{0:T(512)S(1)} copy-done((s32[384]{0:T(512)S(1)}, s32[384]{0:T(512)}, u32[]{:S(2)}) %copy-start.2) | copy-done | bytes 1560
  1.3 0.0 copy-start
  1.3 0.0 copy-done.3
  1.3 0.0 copy-start.1
  1.3 53.5 %network_256.1 = (f32[300,320]{1,0:T(8,128)S(1)}, f32[2,300]{1,0:T(2,128)S(1)}, s32[1]{0:T(128)}) custom-call(s32[1,384]{1,0:T(1,128)S(1)} %reshape.14.resample, f32[320,384]{1,0:T(8,128)} %bitcast.4, s32[300,320]{1,0:T(8,128)} %bitcast.6, f32[1,320]{1,0:T(1,128)S(1)} %reshape.15.ref_kim), custom_call_target="tpu_custom_call" | custom-call | tf_op jit(solution)/shard_map/network_256/pallas_call | solution.py:541
  55.5 0.0 copy-done
  55.5 0.0 copy-done.1
  55.5 0.2 conditional.1
  55.8 0.8 %copy.12 = f32[320,300]{0,1:T(8,128)} copy(f32[320,300]{0,1:T(8,128)S(1)} %bitcast.8) | data formatting | bytes 768000
  56.6 0.6 %copy.13 = f32[2,300]{1,0:T(2,128)} copy(f32[2,300]{1,0:T(2,128)S(1)} %get-tuple-element.37) | data formatting | bytes 4800
  (2 shorter events, 0.0 us)
Async XLA Ops:
  0.6 0.7 %copy-start.2 = (s32[384]{0:T(512)S(1)}, s32[384]{0:T(512)}, u32[]{:S(2)}) copy-start(s32[384]{0:T(512)} %param.7) | copy-start | bytes 4612
  0.6 0.7 %copy-start.3 = (f32[320]{0:T(512)S(1)}, f32[320]{0:T(512)}, u32[]{:S(2)}) copy-start(f32[320]{0:T(512)} %param.9) | copy-start | bytes 3844
  1.3 54.2 %copy-start = (f32[384,320]{0,1:T(8,128)S(1)}, f32[384,320]{0,1:T(8,128)}, u32[]{:S(2)}) copy-start(f32[384,320]{0,1:T(8,128)} %param.6) | copy-start | bytes 1474564
  1.3 54.2 %copy-start.1 = (s32[320,300]{0,1:T(8,128)S(1)}, s32[320,300]{0,1:T(8,128)}, u32[]{:S(2)}) copy-start(s32[320,300]{0,1:T(8,128)} %param.8) | copy-start | bytes 1152004

commit v6 on v5

--- a/solution.py
+++ b/solution.py
@@ -15,6 +15,7 @@
 OWN = 320
 HALF = OWN // 2
 LINE = 4
+OFTEN = 8
 CHUNK = 2 * OWN
 EARLY = 2 * (LINE - 1) * HALF
 LATE = 2 * LINE * HALF
@@ -93,22 +94,26 @@
         ).astype(bf16)
         rank = jnp.dot(present.astype(bf16), before, preferred_element_type=f32)
         place_of = jnp.where(present > 0.5, rank, -1.0)[0:1, :].astype(jnp.int32)
-    else:
-        place_of = lax.broadcasted_iota(jnp.int32, (1, SAMPLES), 1)
-    count_out[0] = jnp.sum(present[0:1, :].astype(jnp.int32))
+        pick = jnp.where(
+            lax.broadcasted_iota(jnp.int32, (depth, SAMPLES), 0) == place_of, 1.0, 0.0
+        ).astype(bf16)
+    often = jnp.where(times > OFTEN + 0.5, float(SAMPLES), 0.0)
+    count_out[0] = jnp.sum((present + often)[0:1, :].astype(jnp.int32))
     times = times[0:1, :]
-    pick = jnp.where(
-        lax.broadcasted_iota(jnp.int32, (depth, SAMPLES), 0) == place_of, 1.0, 0.0
-    ).astype(bf16)
     load_values.wait()
     values = values_in[...]
     mean = jnp.sum(values * times, axis=1, keepdims=True) * (1.0 / SAMPLES)
     centered = values - mean
     total = jnp.sum(centered * centered * times, axis=1, keepdims=True)
     scaled = (centered * lax.rsqrt(total + 1e-06)).astype(bf16)
-    weighted = (scaled.astype(f32) * times).astype(bf16)
-    side = lax.dot_general(weighted, pick, NT, preferred_element_type=f32)
-    front = lax.dot_general(scaled, pick, NT, preferred_element_type=f32)
+    if compact:
+        weighted = (scaled.astype(f32) * times).astype(bf16)
+        side = lax.dot_general(weighted, pick, NT, preferred_element_type=f32)
+        front = lax.dot_general(scaled, pick, NT, preferred_element_type=f32)
+    else:
+        every = jnp.dot(scaled, hits, preferred_element_type=f32)
+        side = jnp.concatenate([every, jnp.zeros((OWN, depth - SAMPLES), f32)], axis=1)
+        front = side
     load_labels.wait()
     marks = labels_in[...].astype(f32)
     module = lax.broadcasted_iota(jnp.int32, (K, depth), 0).astype(f32) - 150.0

time: 57.3 us -> 57.3 us (level)
  no operation moved by 1% of the time
where the time goes in v6:
time: 57.3 us; the launch traced here: 57.1 us
  Pallas kernels  53.5 us (93%)
  local copies, waits for them, and re-layouts  2.04 us (4%)
  between operations  1.37 us (2%)
    pallas_call x1, Pallas kernels, whole(): pl.pallas_call(functools.partial(kernel, depth, compact), out_shape=(jax....  53.5 us
    unnamed x10, local copies, waits for them, and re-layouts  2.03 us

profile of v6, /device:TPU:1, one launch (start us, length us, event | category | flops | bytes accessed | tf_op | source)
XLA Modules:
  0.0 57.1 jit_solution(8822343994799948443)
XLA Ops:
  0.6 0.0 copy-start.2
  0.6 0.0 copy-start.3
  0.6 0.7 %copy-done.2 = s32[384]{0:T(512)S(1)} copy-done((s32[384]{0:T(512)S(1)}, s32[384]{0:T(512)}, u32[]{:S(2)}) %copy-start.2) | copy-done | bytes 1560
  1.3 0.0 copy-start
  1.3 0.0 copy-done.3
  1.3 0.0 copy-start.1
  1.3 53.5 %network_256.1 = (f32[300,320]{1,0:T(8,128)S(1)}, f32[2,300]{1,0:T(2,128)S(1)}, s32[1]{0:T(128)}) custom-call(s32[1,384]{1,0:T(1,128)S(1)} %reshape.14.resample, f32[320,384]{1,0:T(8,128)} %bitcast.4, s32[300,320]{1,0:T(8,128)} %bitcast.6, f32[1,320]{1,0:T(1,128)S(1)} %reshape.15.ref_kim), custom_call_target="tpu_custom_call" | custom-call | tf_op jit(solution)/shard_map/network_256/pallas_call | solution.py:546
  55.5 0.0 copy-done
  55.5 0.0 copy-done.1
  55.5 0.2 conditional.1
  55.8 0.8 %copy.12 = f32[320,300]{0,1:T(8,128)} copy(f32[320,300]{0,1:T(8,128)S(1)} %bitcast.8) | data formatting | bytes 768000
  56.6 0.6 %copy.13 = f32[2,300]{1,0:T(2,128)} copy(f32[2,300]{1,0:T(2,128)S(1)} %get-tuple-element.37) | data formatting | bytes 4800
  (2 shorter events, 0.0 us)
Async XLA Ops:
  0.6 0.7 %copy-start.2 = (s32[384]{0:T(512)S(1)}, s32[384]{0:T(512)}, u32[]{:S(2)}) copy-start(s32[384]{0:T(512)} %param.7) | copy-start | bytes 4612
  0.6 0.7 %copy-start.3 = (f32[320]{0:T(512)S(1)}, f32[320]{0:T(512)}, u32[]{:S(2)}) copy-start(f32[320]{0:T(512)} %param.9) | copy-start | bytes 3844
  1.3 54.2 %copy-start = (f32[384,320]{0,1:T(8,128)S(1)}, f32[384,320]{0,1:T(8,128)}, u32[]{:S(2)}) copy-start(f32[384,320]{0,1:T(8,128)} %param.6) | copy-start | bytes 1474564
  1.3 54.2 %copy-start.1 = (s32[320,300]{0,1:T(8,128)S(1)}, s32[320,300]{0,1:T(8,128)}, u32[]{:S(2)}) copy-start(s32[320,300]{0,1:T(8,128)} %param.8) | copy-start | bytes 1152004
